TPU v7x, 8 devices: a whole 2x2x1 slice. The times are simulated.
8 devices in a mesh: dp: 1 (over z), tp: 2 (over y), cp: 4 (over x, core).
Axes of the slice: x: 2, y: 2, z: 1, core: 2. Of those that a mesh axis runs over, the one named last changes fastest.
Arguments:
- hidden: bfloat16 [4096, 2048], P(('dp', 'cp'))
- positions: int32 [4096], P(('dp', 'cp'))
- ln_gain: bfloat16 [2048], replicated
- w_q: bfloat16 [2048, 2048], P(None, 'tp')
- w_k: bfloat16 [2048, 1024], P(None, 'tp')
- w_v: bfloat16 [2048, 1024], P(None, 'tp')
- w_o: bfloat16 [2048, 2048], P('tp')
- w_gate: bfloat16 [2048, 6144], P(None, 'tp')
- w_up: bfloat16 [2048, 6144], P(None, 'tp')
- w_down: bfloat16 [6144, 2048], P('tp')
Outputs:
- output 1: bfloat16 [4096, 2048], P(('dp', 'cp'))
- output 2: bfloat16 [4096, 8, 128], P(('dp', 'cp'), 'tp')
- output 3: bfloat16 [4096, 8, 128], P(('dp', 'cp'), 'tp')
All inputs are finite; a program needn't handle non-finite values.
Results may differ from a plain program's by a relative error of at most 0.012868.
Values are sent between devices in bfloat16 or wider.
A program may use at most 1 GiB of HBM per device.

v0:
```python
import jax
import jax.numpy as jnp
from jax import lax
from jax.sharding import PartitionSpec as P

HEAD_DIM = 128
ROPE_BASE = 4000000
LN_EPS = 1e-5


def layer_norm(hidden, ln_gain):
    hidden_f = hidden.astype(jnp.float32)
    row_mean = jnp.mean(hidden_f, axis=-1, keepdims=True)
    centered = hidden_f - row_mean
    row_var = jnp.mean(centered * centered, axis=-1, keepdims=True)
    return (centered * lax.rsqrt(row_var + LN_EPS) * ln_gain.astype(jnp.float32)).astype(jnp.bfloat16)


def rotary(proj, positions):
    half_dim = HEAD_DIM // 2
    inv_freq = 1.0 / (ROPE_BASE ** (jnp.arange(0, HEAD_DIM, 2, dtype=jnp.float32) / HEAD_DIM))
    angles = positions.astype(jnp.float32)[:, None] * inv_freq[None, :]
    bcast_shape = (proj.shape[0],) + (1,) * (proj.ndim - 2) + (half_dim,)
    cosine = jnp.cos(angles).reshape(bcast_shape)
    sine_val = jnp.sin(angles).reshape(bcast_shape)
    paired = proj.astype(jnp.float32).reshape(proj.shape[:-1] + (half_dim, 2))
    even_part = paired[..., 0]
    odd_part = paired[..., 1]
    rotated = jnp.stack([even_part * cosine - odd_part * sine_val, odd_part * cosine + even_part * sine_val], axis=-1)
    return rotated.reshape(proj.shape).astype(jnp.bfloat16)


def attend_all(q_rot, k_all, v_all, my_block):
    tok_rows, kv_local, group_size, head_dim = q_rot.shape
    score_scale = head_dim ** -0.5
    query_pos = my_block * tok_rows + jnp.arange(tok_rows)

    def key_step(src_block, loop_state):
        row_max, row_sum, accum = loop_state
        k_block = lax.dynamic_index_in_dim(k_all, src_block, 0, keepdims=False)
        v_block = lax.dynamic_index_in_dim(v_all, src_block, 0, keepdims=False)
        scores = jnp.einsum('qkgd,tkd->kqgt', q_rot, k_block, preferred_element_type=jnp.float32) * score_scale
        key_pos = src_block * tok_rows + jnp.arange(tok_rows)
        allowed = (key_pos[None, :] <= query_pos[:, None])[None, :, None, :]
        scores = jnp.where(allowed, scores, -jnp.inf)
        new_max = jnp.maximum(row_max, jnp.max(scores, axis=-1))
        weights = jnp.exp(scores - new_max[..., None])
        factor = jnp.exp(row_max - new_max)
        new_sum = row_sum * factor + jnp.sum(weights, axis=-1)
        new_accum = accum * factor[..., None] + jnp.einsum('kqgt,tkd->kqgd', weights.astype(jnp.bfloat16), v_block, preferred_element_type=jnp.float32)
        return new_max, new_sum, new_accum

    state_shape = (kv_local, tok_rows, group_size)
    init_state = (jnp.full(state_shape, -jnp.inf, jnp.float32), jnp.zeros(state_shape, jnp.float32), jnp.zeros(state_shape + (head_dim,), jnp.float32))
    row_max, row_sum, accum = lax.fori_loop(0, my_block + 1, key_step, init_state)
    attn = (accum / row_sum[..., None]).astype(jnp.bfloat16)
    return jnp.transpose(attn, (1, 0, 2, 3)).reshape(tok_rows, kv_local * group_size * head_dim)


def solution(mesh):
    def local_layer(hidden, positions, ln_gain, w_q, w_k, w_v, w_o, w_gate, w_up, w_down):
        tok_rows = hidden.shape[0]
        kv_local = w_k.shape[1] // HEAD_DIM
        group_size = w_q.shape[1] // w_k.shape[1]
        my_block = lax.axis_index('cp')
        normed = layer_norm(hidden, ln_gain)
        q_proj = jnp.dot(normed, w_q, preferred_element_type=jnp.float32).astype(jnp.bfloat16)
        k_proj = jnp.dot(normed, w_k, preferred_element_type=jnp.float32).astype(jnp.bfloat16)
        v_cache = jnp.dot(normed, w_v, preferred_element_type=jnp.float32).astype(jnp.bfloat16).reshape(tok_rows, kv_local, HEAD_DIM)
        q_rot = rotary(q_proj.reshape(tok_rows, kv_local, group_size, HEAD_DIM), positions)
        k_cache = rotary(k_proj.reshape(tok_rows, kv_local, HEAD_DIM), positions)
        k_all = lax.all_gather(k_cache, 'cp')
        v_all = lax.all_gather(v_cache, 'cp')
        attn = attend_all(q_rot, k_all, v_all, my_block)
        attn_part = jnp.dot(attn, w_o, preferred_element_type=jnp.float32).astype(jnp.bfloat16)
        attn_sum = lax.psum(attn_part, 'tp')
        gate_proj = jnp.dot(normed, w_gate, preferred_element_type=jnp.float32).astype(jnp.bfloat16)
        up_proj = jnp.dot(normed, w_up, preferred_element_type=jnp.float32).astype(jnp.bfloat16)
        mlp_act = (jax.nn.silu(gate_proj.astype(jnp.float32)) * up_proj.astype(jnp.float32)).astype(jnp.bfloat16)
        mlp_part = jnp.dot(mlp_act, w_down, preferred_element_type=jnp.float32).astype(jnp.bfloat16)
        mlp_sum = lax.psum(mlp_part, 'tp')
        hidden_out = (hidden.astype(jnp.float32) + attn_sum.astype(jnp.float32) + mlp_sum.astype(jnp.float32)).astype(jnp.bfloat16)
        return hidden_out, k_cache, v_cache

    row_spec = P(('dp', 'cp'), None)
    col_spec = P(None, 'tp')
    cache_spec = P(('dp', 'cp'), 'tp', None)
    in_specs = (row_spec, P(('dp', 'cp')), P(None), col_spec, col_spec, col_spec, P('tp', None), col_spec, col_spec, P('tp', None))
    return jax.shard_map(local_layer, mesh=mesh, in_specs=in_specs, out_specs=(row_spec, cache_spec, cache_spec), check_vma=False)
```

profile of v0, /device:TPU:0, one launch (start us, length us, event | category | flops | bytes accessed | tf_op | source)
XLA Modules:
  0.0 541.2 jit_solution(6776154352187356551)
XLA Ops:
  7.2 0.0 copy-start
  7.2 0.0 copy-start.11
  7.2 0.0 all-gather.5.cloned.1.call-start
  7.2 0.0 copy-start.2
  7.2 3.0 convert_reduce_fusion
  10.2 0.6 copy-done.2
  10.8 1.2 fusion.26
  12.1 0.0 copy-done.11
  12.1 1.6 fusion.28
  13.7 0.0 copy-done
  13.7 0.0 copy-start.7
  13.8 0.0 copy-start.12
  13.8 2.4 convolution_convert_fusion.1
  16.1 0.0 copy-done.7
  16.2 0.0 copy-start.9
  16.2 1.3 copy.36
  17.5 0.0 all-gather.5.cloned.1.call-update
  17.5 0.6 all-gather.3.cloned.1.call-start
  18.1 0.0 copy-done.12
  18.1 6.6 %fusion.38 = f32[1024,512]{0,1:T(8,128)} fusion(bf16[1024,2048]{1,0:T(8,128)(2,1)} %copy-done.7, bf16[2048,512]{1,0:T(8,128)(2,1)} %param.16), kind=kOutput, calls=%fused_computation.52 | convolution fusion | flops 2148532224 | bytes 8388608 | tf_op jit(solution)/shard_map/dot_general | solution.py:68
  24.7 0.0 copy-done.9
  24.7 2.5 reshape.183
  27.2 1.0 multiply_cosine_fusion
  28.2 1.6 fusion.41
  29.8 1.6 multiply_subtract_fusion
  31.4 0.7 maximum_convert_fusion
  32.1 0.0 copy-start.5
  32.1 1.7 copy.33
  33.8 0.0 all-gather.3.cloned.1.call-update
  33.9 0.2 all-reduce.3.cloned.1.call-start
  34.1 10.0 %convert_convert_fusion = f32[1024,1024]{0,1:T(8,128)} fusion(bf16[1024,2048]{1,0:T(8,128)(2,1)} %copy-done.7, bf16[2048,1024]{1,0:T(8,128)(2,1)} %param.15), kind=kOutput, calls=%fused_computation.49 | convolution fusion | flops 4297064448 | bytes 12582912 | tf_op jit(solution)/shard_map/dot_general | solution.py:67
  44.1 0.0 copy-done.5
  44.1 5.8 %reshape.184 = f32[1024,4,2,64,2]{0,4,3,2,1:T(2,128)} reshape(f32[1024,1024]{0,1:T(8,128)} %convert_convert_fusion) | data formatting | bytes 8388608 | tf_op jit(solution)/shard_map/convert_element_type | solution.py:26
  49.9 7.7 %fusion.40 = (f32[1024,4,2,64,1]{0,4,3,2,1:T(1,128)S(1)}, f32[1024,4,2,64,1]{0,4,3,2,1:T(1,128)S(1)}) fusion(f32[1024,4,2,64,2]{0,4,3,2,1:T(2,128)} %reshape.184), kind=kLoop, calls=%fused_computation.61 | loop fusion | bytes 8388608 | tf_op jit(solution)/shard_map/slice | solution.py:27
  57.6 0.0 copy-done.8
  57.6 17.2 %fusion.42 = bf16[1024,3072]{1,0:T(8,128)(2,1)} fusion(bf16[1024,2048]{1,0:T(8,128)(2,1)S(1)} %copy-done.8, bf16[2048,3072]{1,0:T(8,128)(2,1)} %param.19), kind=kOutput, calls=%fused_computation.63 | convolution fusion | flops 12884901888 | bytes 23068672 | tf_op jit(solution)/shard_map/dot_general | solution.py:77
  74.8 3.4 subtract_convert_fusion
  78.3 2.7 pad_maximum_fusion
  81.0 4.0 copy.37
  84.9 38.3 %fusion.35 = bf16[1024,2048]{1,0:T(8,128)(2,1)} fusion(bf16[3072,2048]{1,0:T(8,128)(2,1)} %param.21, bf16[1024,3072]{1,0:T(8,128)(2,1)} %fusion.42, bf16[1024,2048]{1,0:T(8,128)(2,1)} %copy-done.7, bf16[2048,3072]{1,0:T(8,128)(2,1)} %param.20), kind=kOutput, calls=%fused_computation.44 | convolution fusion | flops 25800212480 | bytes 39845888 | tf_op jit(solution)/shard_map/dot_general | solution.py:80
  123.3 0.0 all-gather.5.cloned.1.call-done
  123.3 0.0 all-gather.3.cloned.1.call-done
  123.4 2.4 broadcast_in_dim.16
  125.7 47.2 %while.15 = (s32[]{:T(128)}, f32[4,1024,2]{1,2,0:T(2,128)S(1)}, f32[4,1024,2]{1,2,0:T(2,128)S(1)}, f32[4,1024,2,128]{3,1,2,0:T(8,128)}, s32[]{:T(128)}, /*index=...) while((s32[]{:T(128)}, f32[4,1024,2]{1,2,0:T(2,128)S(1)}, ...), condition=%wide.region_5.6_spmd.clone, body=%wide.region_2.5_spmd.clone.sunk | while | flops 4390406144 | bytes 151535856 | solution.py:55
  125.7 0.7 broadcast_compare_fusion.2
  126.4 15.0 %fusion.65 = (f32[4,1024,2]{1,2,0:T(2,128)S(1)}, f32[4,1024,1024,2]{2,1,3,0:T(8,128)}) fusion(pred[1024,1024]{0,1:T(8,128)(4,1)S(1)} %broadcast_compare_fusion.2, bf16[1024,4,2,128]{3,0,2,1:T(8,128)(2,1)} %get-tuple-element.243, bf16[4,1024,4,128]{3,1,2,0:T(8,128)(2,1)} %get-tuple-element.242, s32[]{:T(128)S(6)} %select_n.28), kind=kOutput, calls=%fused_computation.5.clone.1 | convolution fusion | flops 2172641280 | bytes 37781508 | tf_op jit(solution)/shard_map/while/body/qkgd,tkd->kqgt/dot_general | solution.py:42
  141.4 0.0 copy-start.3
  141.4 14.5 %fusion.66 = f32[4,1024,2]{1,2,0:T(2,128)S(1)} fusion(f32[4,1024,1024,2]{2,1,3,0:T(8,128)} %get-tuple-element.208, f32[4,1024,2]{1,2,0:T(2,128)S(1)} %max.5, pred[1024,1024]{0,1:T(8,128)(4,1)S(1)} %broadcast_compare_fusion.2), kind=kLoop, calls=%fused_computation.4.clone.1 | loop fusion | flops 33546240 | bytes 34668544 | tf_op jit(solution)/shard_map/while/body/reduce_sum | solution.py:49
  155.9 0.0 copy-done.3
  155.9 15.0 %multiply_add_fusion.6 = f32[4,1024,2,128]{3,1,2,0:T(8,128)S(1)} fusion(f32[4,1024,2,128]{3,1,2,0:T(8,128)S(1)} %copy-done.3, f32[4,1024,1024,2]{2,1,3,0:T(8,128)} %get-tuple-element.208, f32[4,1024,2]{1,2,0:T(2,128)S(1)} %max.5, pred[1024,1024]{0,1:T(8,128)(4,1)S(1)} %broadcast_compare_fusion.2, f32[4,1024,2]{1,2,0:T(2,128)S(1)} %bitcast.92, ...), kind=kOutput, calls=%fused_computation.8.clone.1 | convolution fusion | flops 2183135232 | bytes 44105732 | tf_op jit(solution)/shard_map/while/body/kqgt,tkd->kqgd/dot_general | solution.py:50
  170.9 0.0 copy-start.4
  170.9 2.0 copy-done.4
  172.9 5.4 copy.38
  178.3 3.0 divide_convert_fusion
  181.3 0.5 copy-done.13
  181.8 6.2 %convolution_convert_fusion = bf16[1024,2048]{1,0:T(8,128)(2,1)} fusion(bf16[1024,1024]{0,1:T(8,128)(2,1)S(1)} %bitcast.89, bf16[1024,2048]{1,0:T(8,128)(2,1)S(1)} %copy-done.13), kind=kOutput, calls=%fused_computation.43 | convolution fusion | flops 4297064448 | bytes 10485760 | tf_op jit(solution)/shard_map/dot_general | solution.py:75
  188.0 0.0 all-reduce.3.cloned.1.call-update
  188.0 1.2 copy-done.10
  189.2 1.4 copy.40
  190.6 0.0 copy-done.6
  190.6 2.3 copy.39
  192.9 331.4 %all-reduce.3.cloned.1.call-done = (bf16[1024,2048]{1,0:T(8,128)(2,1)}, bf16[1024,2048]{1,0:T(8,128)(2,1)}) async-done(((bf16[1024,2048]{1,0:T(8,128)(2,1)}, bf16[1024,2048]{1,0:T(8,128)(2,1)}), (bf16[1024,2048]{1,0:T(8,128)(2,1)}, bf16[1024,2048]{1,0:T(8,128)(2,1)})) %all-reduce.3.cloned.1.call-update) | async-done | bytes 8388624 | tf_op jit(solution)/shard_map/psum | solution.py:81
  524.3 10.2 %fusion.30 = bf16[1024,2048]{1,0:T(8,128)(2,1)} fusion(bf16[1024,2048]{1,0:T(8,128)(2,1)} %param.12, bf16[1024,2048]{1,0:T(8,128)(2,1)} %get-tuple-element.121, bf16[1024,2048]{1,0:T(8,128)(2,1)} %get-tuple-element.122), kind=kLoop, calls=%fused_computation.39 | loop fusion | flops 12582912 | bytes 16777216 | tf_op jit(solution)/shard_map/convert_element_type | solution.py:82
  534.5 0.0 copy-done.1
  (16 shorter events, 0.1 us)
Async XLA Ops:
  7.2 6.6 %copy-start = (bf16[2048,512]{1,0:T(8,128)(2,1)S(1)}, bf16[2048,512]{1,0:T(8,128)(2,1)}, u32[]{:S(2)}) copy-start(bf16[2048,512]{1,0:T(8,128)(2,1)} %param.17) | copy-start | bytes 6291460
  7.2 4.9 copy-start.11
  7.2 116.1 %all-gather.5.cloned.1.call-start = ((), (), s32[]{:S(2)}) async-start(), calls=%async_computation.1 | async-start | bytes 5242880 | tf_op jit(solution)/shard_map/all_gather | solution.py:73
  7.2 3.6 copy-start.2
  13.7 2.4 copy-start.7
  13.8 4.3 copy-start.12
  16.2 8.5 %copy-start.9 = (bf16[1024,512]{0,1:T(8,128)(2,1)}, bf16[1024,512]{0,1:T(8,128)(2,1)S(1)}, u32[]{:S(2)}) copy-start(bf16[1024,512]{0,1:T(8,128)(2,1)S(1)} %convolution_convert_fusion.1) | copy-start | bytes 3145732
  17.5 105.8 %all-gather.3.cloned.1.call-start = ((), (), s32[]{:S(2)}) async-start(), calls=%async_computation | async-start | bytes 5242880 | tf_op jit(solution)/shard_map/all_gather | solution.py:72
  32.1 12.0 %copy-start.5 = (bf16[1024,4,64,2]{0,1,3,2:T(4,128)(2,1)}, bf16[1024,4,64,2]{0,1,3,2:T(4,128)(2,1)S(1)}, u32[]{:S(2)}) copy-start(bf16[1024,4,64,2]{0,1,3,2:T(4,128)(2,1)S(1)} %maximum_convert_fusion) | copy-start | bytes 3145732
  33.9 490.4 %all-reduce.3.cloned.1.call-start = ((), (), s32[]{:S(2)}) async-start(), calls=%async_computation.2 | async-start | bytes 16777216 | tf_op jit(solution)/shard_map/psum | solution.py:81
  49.9 7.7 %copy-start.8 = (bf16[1024,2048]{1,0:T(8,128)(2,1)S(1)}, bf16[1024,2048]{1,0:T(8,128)(2,1)}, u32[]{:S(2)}) copy-start(bf16[1024,2048]{1,0:T(8,128)(2,1)} %copy-done.7) | copy-start | bytes 12582916
  141.4 14.5 %copy-start.3 = (f32[4,1024,2,128]{3,1,2,0:T(8,128)S(1)}, f32[4,1024,2,128]{3,1,2,0:T(8,128)}, u32[]{:S(2)}) copy-start(f32[4,1024,2,128]{3,1,2,0:T(8,128)} %get-tuple-element.227) | copy-start | bytes 12582916 | tf_op jit(solution)/shard_map/while
  170.9 2.0 copy-start.4
  178.3 3.4 copy-start.13
  188.0 1.2 copy-start.10
  188.0 2.7 copy-start.6
  524.3 10.2 %copy-start.1 = (bf16[2048,512]{1,0:T(8,128)(2,1)S(1)}, bf16[2048,512]{1,0:T(8,128)(2,1)}, u32[]{:S(2)}) copy-start(bf16[2048,512]{1,0:T(8,128)(2,1)} %param.17) | copy-start | bytes 6291460
Sparse Core Ops, SparseCore 0:
  17.6 34.3 all-gather.4
  54.1 31.4 all-gather.2
  188.1 336.1 all-reduce.2
where the time goes:
time: 546 us; the launch traced here: 541 us
  waiting for transfers between devices  331 us (61%)
  matrix products  111 us (20%)
  other arithmetic  43.5 us (8%)
  local copies, waits for them, and re-layouts  40.4 us (7%)
  between operations  14.2 us (3%)
    psum x1, waiting for transfers between devices, local_layer(): mlp_sum = lax.psum(mlp_part, 'tp')  331 us
    dot_general x1, matrix products, local_layer(): jnp.dot(mlp_act, w_down, preferred_element_type=jnp.float32)  38.3 us
    dot_general x1, matrix products, local_layer(): jnp.dot(normed, w_gate, preferred_element_type=jnp.float32)  17.2 us
    dot_general x1, matrix products, key_step(): jnp.einsum('qkgd,tkd->kqgt', q_rot, k_block, preferred_element_type=jnp.f...  15 us
    dot_general x1, matrix products, key_step(): jnp.einsum('kqgt,tkd->kqgd', weights.astype(jnp.bfloat16), v_block, prefe...  15 us
    reduce_sum x1, other arithmetic, key_step(): new_sum = row_sum * factor + jnp.sum(weights, axis=-1)  14.5 us
  transfers between devices with their start and end apart: 3, of which 1 were waited for; matrix products, arithmetic and copies ran while one was open for 20% of the time, Pallas kernels for 0%

commit v1 on v0

v1 whole, which is shorter than its diff:
```python
import functools
import math

import jax
import jax.numpy as jnp
from jax import lax
from jax.experimental import pallas as pl
from jax.experimental.pallas import tpu as pltpu
from jax.sharding import PartitionSpec as P


HEAD_DIM = 128
ROPE_BASE = 4000000
LN_EPS = 1e-5
F32 = jnp.float32
BF16 = jnp.bfloat16
VMEM_LIMIT = 67043328
CHUNKS = (128, 256, 256, 256, 128)


def params(*semantics):
    return pltpu.CompilerParams(dimension_semantics=semantics, vmem_limit_bytes=VMEM_LIMIT)


def cost(flops, nbytes):
    return pl.CostEstimate(flops=int(flops), bytes_accessed=int(nbytes), transcendentals=0)


def norm_v_kernel(x_ref, g_ref, wv_ref, h_ref, v_ref, vt_ref):
    x = x_ref[...].astype(F32)
    mean = jnp.mean(x, axis=-1, keepdims=True)
    cent = x - mean
    var = jnp.mean(cent * cent, axis=-1, keepdims=True)
    h = (cent * lax.rsqrt(var + LN_EPS) * g_ref[...].astype(F32)).astype(BF16)
    h_ref[...] = h
    v = jnp.dot(h, wv_ref[...], preferred_element_type=F32).astype(BF16)
    v_ref[...] = v
    vt_ref[...] = v.T


def norm_v(hidden, gain, w_v):
    rows, width = hidden.shape
    cols = w_v.shape[1]
    blk = 256
    return pl.pallas_call(
        norm_v_kernel,
        grid=(rows // blk,),
        in_specs=[
            pl.BlockSpec((blk, width), lambda i: (i, 0)),
            pl.BlockSpec((1, width), lambda i: (0, 0)),
            pl.BlockSpec((width, cols), lambda i: (0, 0)),
        ],
        out_specs=[
            pl.BlockSpec((blk, width), lambda i: (i, 0)),
            pl.BlockSpec((blk, cols), lambda i: (i, 0)),
            pl.BlockSpec((cols, blk), lambda i: (0, i)),
        ],
        out_shape=[
            jax.ShapeDtypeStruct((rows, width), BF16),
            jax.ShapeDtypeStruct((rows, cols), BF16),
            jax.ShapeDtypeStruct((cols, rows), BF16),
        ],
        compiler_params=params("arbitrary"),
        cost_estimate=cost(2 * rows * width * cols, 4 * rows * width + 2 * width * cols),
        name="norm_v",
    )(hidden, gain.reshape(1, width), w_v)


def rope_proj_kernel(h_ref, w_ref, cos_ref, sin_ref, swap_ref, out_ref):
    proj = jnp.dot(h_ref[...], w_ref[...], preferred_element_type=F32).astype(BF16)
    swapped = jnp.dot(proj, swap_ref[...], preferred_element_type=F32)
    cos = cos_ref[...]
    sin = sin_ref[...]
    for j in range(proj.shape[1] // HEAD_DIM):
        cols = slice(j * HEAD_DIM, (j + 1) * HEAD_DIM)
        out_ref[:, cols] = (proj[:, cols].astype(F32) * cos + swapped[:, cols] * sin).astype(BF16)


def rope_proj(h, w, cos, sin, swap):
    rows, width = h.shape
    cols = w.shape[1]
    blk = 256
    return pl.pallas_call(
        rope_proj_kernel,
        grid=(cols // blk,),
        in_specs=[
            pl.BlockSpec((rows, width), lambda i: (0, 0)),
            pl.BlockSpec((width, blk), lambda i: (0, i)),
            pl.BlockSpec((rows, HEAD_DIM), lambda i: (0, 0)),
            pl.BlockSpec((rows, HEAD_DIM), lambda i: (0, 0)),
            pl.BlockSpec((blk, blk), lambda i: (0, 0)),
        ],
        out_specs=pl.BlockSpec((rows, blk), lambda i: (0, i)),
        out_shape=jax.ShapeDtypeStruct((rows, cols), BF16),
        compiler_params=params("arbitrary"),
        cost_estimate=cost(2 * rows * width * cols, 2 * rows * (width + cols) + 2 * width * cols),
    )(h, w, cos, sin, swap)


def gate_up_kernel(h_ref, wg_ref, wu_ref, *refs):
    h = h_ref[...]
    gate = jnp.dot(h, wg_ref[...], preferred_element_type=F32).astype(BF16).astype(F32)
    up = jnp.dot(h, wu_ref[...], preferred_element_type=F32).astype(BF16).astype(F32)
    refs[-1][...] = (jax.nn.silu(gate) * up).astype(BF16)


def gate_up(h, w_gate, w_up, first, last, out):
    rows, width = h.shape
    cols = w_gate.shape[1]
    blk = 256
    specs = [
        pl.BlockSpec((rows, width), lambda i: (0, 0)),
        pl.BlockSpec((width, blk), lambda i: (0, first + i)),
        pl.BlockSpec((width, blk), lambda i: (0, first + i)),
    ]
    operands = [h, w_gate, w_up]
    aliases = {}
    if out is not None:
        specs.append(pl.BlockSpec(memory_space=pl.ANY))
        operands.append(out)
        aliases = {3: 0}
    done = (last - first) * blk
    return pl.pallas_call(
        gate_up_kernel,
        grid=(last - first,),
        in_specs=specs,
        out_specs=pl.BlockSpec((rows, blk), lambda i: (0, first + i)),
        out_shape=jax.ShapeDtypeStruct((rows, cols), BF16),
        input_output_aliases=aliases,
        compiler_params=params("arbitrary"),
        cost_estimate=cost(4 * rows * width * done, 2 * rows * (width + done) + 4 * width * done),
        name="gate_up",
    )(*operands)


def chunk_kernel(row0, rows, q_ref, k0, v0, k1, v1, k2, v2, k3, v3, a_ref, wo_ref, wd_ref,
                 out_ref, max_ref, sum_ref, acc_ref, part_ref):
    step = pl.program_id(0)
    me = lax.axis_index("cp")
    scale = HEAD_DIM ** -0.5 * math.log2(math.e)
    q = jnp.concatenate([q_ref[:, :HEAD_DIM], q_ref[:, HEAD_DIM:]], axis=0)

    def scores(k):
        return lax.dot_general(k, q, (((1,), (1,)), ((), ())), preferred_element_type=F32) * scale

    diag = scores(k0[row0:row0 + rows, :])
    key_id = lax.broadcasted_iota(jnp.int32, diag.shape, 0)
    query_id = lax.broadcasted_iota(jnp.int32, diag.shape, 1) % rows
    diag = jnp.where(key_id <= query_id, diag, -jnp.inf)
    top = jnp.max(diag, axis=0, keepdims=True)
    if row0:
        rest = scores(k0[:row0, :])
        top = jnp.maximum(top, jnp.max(rest, axis=0, keepdims=True))
    weight = jnp.exp2(diag - top)
    total = jnp.sum(weight, axis=0, keepdims=True)
    acc = jnp.dot(v0[:, row0:row0 + rows], weight.astype(BF16), preferred_element_type=F32)
    if row0:
        weight = jnp.exp2(rest - top)
        total += jnp.sum(weight, axis=0, keepdims=True)
        acc += jnp.dot(v0[:, :row0], weight.astype(BF16), preferred_element_type=F32)
    max_ref[...] = top
    sum_ref[...] = total
    acc_ref[...] = acc

    def other(k_ref, v_ref):
        s = scores(k_ref[...])
        old = max_ref[...]
        new = jnp.maximum(old, jnp.max(s, axis=0, keepdims=True))
        factor = jnp.exp2(old - new)
        weight = jnp.exp2(s - new)
        sum_ref[...] = sum_ref[...] * factor + jnp.sum(weight, axis=0, keepdims=True)
        acc_ref[...] = acc_ref[...] * factor + jnp.dot(v_ref[...], weight.astype(BF16), preferred_element_type=F32)
        max_ref[...] = new

    @pl.when(me % 2 == 1)
    def _():
        other(k1, v1)

    @pl.when(me >= 2)
    def _():
        other(k2, v2)
        other(k3, v3)

    o = (acc_ref[...] / sum_ref[...]).T.astype(BF16)
    o = jnp.concatenate([o[:rows, :], o[rows:, :]], axis=1)
    part = jnp.dot(o, wo_ref[...], preferred_element_type=F32)
    part += jnp.dot(a_ref[...], wd_ref[...], preferred_element_type=F32)

    @pl.when(step == 0)
    def _():
        part_ref[...] = part

    @pl.when(step > 0)
    def _():
        part_ref[...] += part

    @pl.when(step == pl.num_programs(0) - 1)
    def _():
        out_ref[...] = part_ref[...].astype(BF16)


def chunk_part(row0, rows, q, sources, act, w_o, w_down):
    tok_rows = q.shape[0]
    kv_heads = q.shape[1] // (2 * HEAD_DIM)
    width = w_o.shape[1]
    ff_blk = act.shape[1] // kv_heads
    q = q[row0:row0 + rows]
    act = act[row0:row0 + rows]
    kv_specs = []
    operands = []
    for k, vt in sources:
        kv_specs += [pl.BlockSpec((tok_rows, HEAD_DIM), lambda g: (0, g)), pl.BlockSpec((HEAD_DIM, tok_rows), lambda g: (g, 0))]
        operands += [k, vt]
    return pl.pallas_call(
        functools.partial(chunk_kernel, row0, rows),
        grid=(kv_heads,),
        in_specs=[pl.BlockSpec((rows, 2 * HEAD_DIM), lambda g: (0, g))] + kv_specs + [
            pl.BlockSpec((rows, ff_blk), lambda g: (0, g)),
            pl.BlockSpec((2 * HEAD_DIM, width), lambda g: (g, 0)),
            pl.BlockSpec((ff_blk, width), lambda g: (g, 0)),
        ],
        out_specs=pl.BlockSpec((rows, width), lambda g: (0, 0)),
        out_shape=jax.ShapeDtypeStruct((rows, width), BF16),
        scratch_shapes=[
            pltpu.VMEM((1, 2 * rows), F32),
            pltpu.VMEM((1, 2 * rows), F32),
            pltpu.VMEM((HEAD_DIM, 2 * rows), F32),
            pltpu.VMEM((rows, width), F32),
        ],
        compiler_params=params("arbitrary"),
        cost_estimate=cost(2 * rows * (width * (act.shape[1] + q.shape[1]) + 8 * tok_rows * q.shape[1]), 30e6),
        name="chunk_part",
    )(q, *operands, act, w_o, w_down)


def add_kernel(x_ref, p_ref, r_ref, *refs):
    refs[-1][...] = (x_ref[...].astype(F32) + (p_ref[...].astype(F32) + r_ref[...].astype(F32))).astype(BF16)


def add_chunk(row0, hidden, part, recv, out):
    rows, width = part.shape
    blk = 128
    first = row0 // blk
    specs = [
        pl.BlockSpec((blk, width), lambda i: (first + i, 0)),
        pl.BlockSpec((blk, width), lambda i: (i, 0)),
        pl.BlockSpec((blk, width), lambda i: (i, 0)),
    ]
    operands = [hidden, part, recv]
    aliases = {}
    if out is not None:
        specs.append(pl.BlockSpec(memory_space=pl.ANY))
        operands.append(out)
        aliases = {3: 0}
    return pl.pallas_call(
        add_kernel,
        grid=(rows // blk,),
        in_specs=specs,
        out_specs=pl.BlockSpec((blk, width), lambda i: (first + i, 0)),
        out_shape=jax.ShapeDtypeStruct(hidden.shape, BF16),
        input_output_aliases=aliases,
        compiler_params=params("arbitrary"),
        cost_estimate=cost(4 * rows * width, 8 * rows * width),
        name="add_chunk",
    )(*operands)


def rope_tables(positions):
    lane = jnp.arange(HEAD_DIM)
    exponent = (lane - lane % 2).astype(F32) / HEAD_DIM
    inv_freq = 1.0 / (ROPE_BASE ** exponent)
    angles = positions.astype(F32)[:, None] * inv_freq[None, :]
    sign = jnp.where(lane % 2 == 0, -1.0, 1.0).astype(F32)
    return jnp.cos(angles), jnp.sin(angles) * sign[None, :]


def solution(mesh):
    def layer(hidden, positions, ln_gain, w_q, w_k, w_v, w_o, w_gate, w_up, w_down):
        tok_rows = hidden.shape[0]
        kv_local = w_k.shape[1] // HEAD_DIM
        cross = lambda t: lax.ppermute(t, 'cp', [(0, 2), (1, 3)])
        upward = lambda t: lax.ppermute(t, 'cp', [(0, 1), (2, 3)])
        relay = lambda t: lax.ppermute(t, 'cp', [(2, 3), (3, 2)])

        h, v, vt = norm_v(hidden, ln_gain, w_v)
        vt_x = cross(vt)
        positions, h = lax.optimization_barrier((positions, h))
        cos, sin = rope_tables(positions)
        row = jnp.arange(2 * HEAD_DIM)
        swap = (row[:, None] == (row ^ 1)[None, :]).astype(BF16)
        k = rope_proj(h, w_k, cos, sin, swap)
        k_x = cross(k)
        h, k = lax.optimization_barrier((h, k))
        vt_u = upward(vt)
        k_u = upward(k)
        q = rope_proj(h, w_q, cos, sin, swap)
        h, q = lax.optimization_barrier((h, q))
        act = gate_up(h, w_gate, w_up, 0, 6, None)
        vt_r = relay(vt_x)
        act = gate_up(h, w_gate, w_up, 6, 12, act)
        k_r = relay(k_x)
        sources = ((k, vt), (k_u, vt_u), (k_x, vt_x), (k_r, vt_r))
        parts = []
        row0 = 0
        for rows in CHUNKS:
            part = chunk_part(row0, rows, q, sources, act, w_o, w_down)
            recv = lax.ppermute(part, 'tp', [(0, 1), (1, 0)])
            q, part, act = lax.optimization_barrier((q, part, act))
            parts.append((row0, part, recv))
            row0 += rows
        out = None
        for row0, part, recv in parts:
            out = add_chunk(row0, hidden, part, recv, out)
        shape = (tok_rows, kv_local, HEAD_DIM)
        return out, k.reshape(shape), v.reshape(shape)

    row_spec = P(('dp', 'cp'), None)
    col_spec = P(None, 'tp')
    cache_spec = P(('dp', 'cp'), 'tp', None)
    in_specs = (row_spec, P(('dp', 'cp')), P(None), col_spec, col_spec, col_spec, P('tp', None), col_spec, col_spec, P('tp', None))
    return jax.shard_map(layer, mesh=mesh, in_specs=in_specs, out_specs=(row_spec, cache_spec, cache_spec), check_vma=False)
```

time: 546 us -> 238 us (0.44)
  the two profiles are of different devices: /device:TPU:0 before, /device:TPU:3 now
where the time goes in v1:
time: 238 us
  Pallas kernels  186 us (78%)
  local copies, waits for them, and re-layouts  26.6 us (11%)
  starting transfers between devices  14.9 us (6%)
  waiting for transfers between devices  4.67 us (2%)
  other arithmetic  4.42 us (2%)
    pallas_call x5, Pallas kernels, chunk_part(): pl.pallas_call(functools.partial(chunk_kernel, row0, rows), grid=(kv_head...  113 us
    pallas_call x2, Pallas kernels, gate_up(): pl.pallas_call(gate_up_kernel, grid=(last - first,), in_specs=specs, out_...  35.8 us
    pallas_call x2, Pallas kernels, rope_proj(): pl.pallas_call(rope_proj_kernel, grid=(cols // blk,), in_specs=[pl.BlockS...  16.6 us
    pallas_call x5, Pallas kernels, add_chunk(): pl.pallas_call(add_kernel, grid=(rows // blk,), in_specs=specs, out_specs...  13.2 us
    slice x5, local copies, waits for them, and re-layouts, chunk_part(): act = act[row0:row0 + rows]  12.1 us
    slice x5, local copies, waits for them, and re-layouts, chunk_part(): q = q[row0:row0 + rows]  8.94 us
    pallas_call x1, Pallas kernels, norm_v(): pl.pallas_call(norm_v_kernel, grid=(rows // blk,), in_specs=[pl.BlockSpec...  8.08 us
    ppermute x2, starting transfers between devices, layer(): relay = lambda t: lax.ppermute(t, 'cp', [(2, 3), (3, 2)])  5.53 us
  transfers between devices with their start and end apart: 11, of which 1 were waited for; matrix products, arithmetic and copies ran while one was open for 11% of the time, Pallas kernels for 56%

profile of v1, /device:TPU:3, one launch (start us, length us, event | category | flops | bytes accessed | tf_op | source)
XLA Modules:
  0.0 237.5 jit_solution(8523229614074535419)
XLA Ops:
  0.6 1.3 reshape.39.g_ref
  1.9 8.1 %norm_v.1 = (bf16[1024,2048]{1,0:T(8,128)(2,1)}, bf16[1024,512]{1,0:T(8,128)(2,1)}, bf16[512,1024]{1,0:T(8,128)(2,1)}) custom-call(bf16[1024,2048]{1,0:T(8,128)(2,1)} %x_ref.11, bf16[1,2048]{1,0:T(2,128)(2,1)} %reshape.39.g_ref, bf16[2048,512]{1,0:T(8,128)(2,1)} %wv_ref.1), custom_call_target="tpu_custom_call" | custom-call | flops 2147483648 | bytes 10485760 | tf_op jit(solution)/shard_map/norm_v/pallas_call | solution.py:45
  10.0 1.3 collective-permute-start.3
  11.3 1.3 collective-permute-start.1
  12.6 0.7 convert_element_type.15
  13.3 0.7 fusion.1.swap_ref
  14.0 3.0 %fusion = (f32[1024,128]{1,0:T(8,128)}, f32[1024,128]{1,0:T(8,128)}) fusion(f32[128]{0:T(128)S(1)} %get-tuple-element.49, f32[128]{0:T(128)S(1)} %get-tuple-element.50, f32[1024]{0:T(1024)S(1)} %convert_element_type.15), kind=kLoop, calls=%fused_computation.2 | loop fusion | flops 262144 | bytes 1053696 | tf_op jit(solution)/shard_map/mul | solution.py:274
  17.0 6.7 %shard_map.121.k0 = bf16[1024,512]{1,0:T(8,128)(2,1)} custom-call(bf16[1024,2048]{1,0:T(8,128)(2,1)} %get-tuple-element.32.h_ref, bf16[2048,512]{1,0:T(8,128)(2,1)} %w_ref.2, f32[1024,128]{1,0:T(8,128)} %get-tuple-element.48.cos_ref, f32[1024,128]{1,0:T(8,128)} %get-tuple-element.47.sin_ref, bf16[256,256]{1,0:T(8,128)(2,1)} %fusion.1.swap_ref), custom_call_target="tpu_custom_call" | custom-call | flops 2147483648 | bytes 7340032 | tf_op jit(solution)/shard_map/pallas_call | solution.py:83
  23.7 1.3 collective-permute-start.2
  25.0 1.3 collective-permute-start
  26.3 9.8 %shard_map.122 = bf16[1024,1024]{1,0:T(8,128)(2,1)} custom-call(bf16[1024,2048]{1,0:T(8,128)(2,1)} %get-tuple-element.32.h_ref, bf16[2048,1024]{1,0:T(8,128)(2,1)} %w_ref.3, f32[1024,128]{1,0:T(8,128)} %get-tuple-element.48.cos_ref, f32[1024,128]{1,0:T(8,128)} %get-tuple-element.47.sin_ref, bf16[256,256]{1,0:T(8,128)(2,1)} %fusion.1.swap_ref), custom_call_target="tpu_custom_call" | custom-call | flops 4294967296 | bytes 10485760 | tf_op jit(solution)/shard_map/pallas_call | solution.py:83
  36.2 17.9 %gate_up.2.refs_0_ = bf16[1024,3072]{1,0:T(8,128)(2,1)} custom-call(bf16[1024,2048]{1,0:T(8,128)(2,1)} %get-tuple-element.32.h_ref, bf16[2048,3072]{1,0:T(8,128)(2,1)} %wg_ref.3, bf16[2048,3072]{1,0:T(8,128)(2,1)} %wu_ref.3), custom_call_target="tpu_custom_call" | custom-call | flops 12884901888 | bytes 19922944 | tf_op jit(solution)/shard_map/gate_up/pallas_call | solution.py:123
  54.1 4.6 %collective-permute-done.2.k2 = bf16[1024,512]{1,0:T(8,128)(2,1)} collective-permute-done((bf16[1024,512]{1,0:T(8,128)(2,1)}, bf16[1024,512]{1,0:T(8,128)(2,1)}, u32[]{:S(2)}, u32[]{:S(2)}) %collective-permute-start.2) | collective-permute-done | bytes 1048608 | tf_op jit(solution)/shard_map/ppermute | solution.py:281
  58.7 3.4 %collective-permute-start.4 = (bf16[1024,512]{1,0:T(8,128)(2,1)}, bf16[1024,512]{1,0:T(8,128)(2,1)}, u32[]{:S(2)}, u32[]{:S(2)}) collective-permute-start(bf16[1024,512]{1,0:T(8,128)(2,1)} %collective-permute-done.2.k2), channel_id=1, source_target_pairs={{2,3},{3,2},{6,7},{7,6}} | collective-permute-start | bytes 3145736 | tf_op jit(solution)/shard_map/ppermute | solution.py:283
  62.1 0.0 collective-permute-done.3.v2
  62.2 2.1 collective-permute-start.5
  64.3 17.9 %gate_up.3 = bf16[1024,3072]{1,0:T(8,128)(2,1)} custom-call(bf16[1024,2048]{1,0:T(8,128)(2,1)} %get-tuple-element.32.h_ref, bf16[2048,3072]{1,0:T(8,128)(2,1)} %wg_ref.3, bf16[2048,3072]{1,0:T(8,128)(2,1)} %wu_ref.3, bf16[1024,3072]{1,0:T(8,128)(2,1)} %gate_up.2.refs_0_), custom_call_target="tpu_custom_call", output_to_operand_aliasing={{}: (3, {})} | custom-call | flops 12884901888 | bytes 19922944 | tf_op jit(solution)/shard_map/gate_up/pallas_call | solution.py:123
  82.2 2.1 slice.40.a_ref
  84.3 1.7 slice.30.q_ref
  85.9 0.0 collective-permute-done.k1
  85.9 0.0 collective-permute-done.1.v1
  85.9 0.0 collective-permute-done.4.k3
  85.9 0.0 collective-permute-done.5.v3
  86.0 17.3 %chunk_part.5.p_ref = bf16[128,2048]{1,0:T(8,128)(2,1)} custom-call(bf16[128,1024]{1,0:T(8,128)(2,1)} %slice.30.q_ref, bf16[1024,512]{1,0:T(8,128)(2,1)} %shard_map.121.k0, bf16[512,1024]{1,0:T(8,128)(2,1)} %get-tuple-element.31.v0, bf16[1024,512]{1,0:T(8,128)(2,1)} %collective-permute-done.k1, bf16[512,1024]{1,0:T(8,128)(2,1)} %collective-permute-done.1.v1, ...), custom_call_target="tpu_custom_call" | custom-call | flops 4294967296 | bytes 30000000 | tf_op jit(solution)/shard_map/chunk_part/pallas_call | solution.py:214
  103.3 2.7 %slice.33.a_ref = bf16[256,3072]{1,0:T(8,128)(2,1)} slice(bf16[1024,3072]{1,0:T(8,128)(2,1)} %gate_up.3), slice={[128:384], [0:3072]} | slice | bytes 3145728 | tf_op jit(solution)/shard_map/slice | solution.py:208
  105.9 1.9 slice.32.q_ref
  107.8 24.5 %chunk_part.6.p_ref = bf16[256,2048]{1,0:T(8,128)(2,1)} custom-call(bf16[256,1024]{1,0:T(8,128)(2,1)} %slice.32.q_ref, bf16[1024,512]{1,0:T(8,128)(2,1)} %shard_map.121.k0, bf16[512,1024]{1,0:T(8,128)(2,1)} %get-tuple-element.31.v0, bf16[1024,512]{1,0:T(8,128)(2,1)} %collective-permute-done.k1, bf16[512,1024]{1,0:T(8,128)(2,1)} %collective-permute-done.1.v1, ...), custom_call_target="tpu_custom_call" | custom-call | flops 8589934592 | bytes 30000000 | tf_op jit(solution)/shard_map/chunk_part/pallas_call | solution.py:214
  132.3 1.2 collective-permute-start.9
  133.5 2.7 %slice.35.a_ref = bf16[256,3072]{1,0:T(8,128)(2,1)} slice(bf16[1024,3072]{1,0:T(8,128)(2,1)} %gate_up.3), slice={[384:640], [0:3072]} | slice | bytes 3145728 | tf_op jit(solution)/shard_map/slice | solution.py:208
  136.2 1.9 slice.34.q_ref
  138.0 25.5 %chunk_part.7.p_ref = bf16[256,2048]{1,0:T(8,128)(2,1)} custom-call(bf16[256,1024]{1,0:T(8,128)(2,1)} %slice.34.q_ref, bf16[1024,512]{1,0:T(8,128)(2,1)} %shard_map.121.k0, bf16[512,1024]{1,0:T(8,128)(2,1)} %get-tuple-element.31.v0, bf16[1024,512]{1,0:T(8,128)(2,1)} %collective-permute-done.k1, bf16[512,1024]{1,0:T(8,128)(2,1)} %collective-permute-done.1.v1, ...), custom_call_target="tpu_custom_call" | custom-call | flops 8589934592 | bytes 30000000 | tf_op jit(solution)/shard_map/chunk_part/pallas_call | solution.py:214
  163.5 0.2 collective-permute-start.8
  163.7 2.7 %slice.37.a_ref = bf16[256,3072]{1,0:T(8,128)(2,1)} slice(bf16[1024,3072]{1,0:T(8,128)(2,1)} %gate_up.3), slice={[640:896], [0:3072]} | slice | bytes 3145728 | tf_op jit(solution)/shard_map/slice | solution.py:208
  166.4 1.9 slice.36.q_ref
  168.3 26.0 %chunk_part.8.p_ref = bf16[256,2048]{1,0:T(8,128)(2,1)} custom-call(bf16[256,1024]{1,0:T(8,128)(2,1)} %slice.36.q_ref, bf16[1024,512]{1,0:T(8,128)(2,1)} %shard_map.121.k0, bf16[512,1024]{1,0:T(8,128)(2,1)} %get-tuple-element.31.v0, bf16[1024,512]{1,0:T(8,128)(2,1)} %collective-permute-done.k1, bf16[512,1024]{1,0:T(8,128)(2,1)} %collective-permute-done.1.v1, ...), custom_call_target="tpu_custom_call" | custom-call | flops 8589934592 | bytes 30000000 | tf_op jit(solution)/shard_map/chunk_part/pallas_call | solution.py:214
  194.3 1.3 collective-permute-start.7
  195.5 0.2 collective-permute-start.10
  195.7 2.1 slice.39.a_ref
  197.8 1.7 slice.38.q_ref
  199.5 19.3 %chunk_part.9.p_ref = bf16[128,2048]{1,0:T(8,128)(2,1)} custom-call(bf16[128,1024]{1,0:T(8,128)(2,1)} %slice.38.q_ref, bf16[1024,512]{1,0:T(8,128)(2,1)} %shard_map.121.k0, bf16[512,1024]{1,0:T(8,128)(2,1)} %get-tuple-element.31.v0, bf16[1024,512]{1,0:T(8,128)(2,1)} %collective-permute-done.k1, bf16[512,1024]{1,0:T(8,128)(2,1)} %collective-permute-done.1.v1, ...), custom_call_target="tpu_custom_call" | custom-call | flops 4294967296 | bytes 30000000 | tf_op jit(solution)/shard_map/chunk_part/pallas_call | solution.py:214
  218.8 1.3 collective-permute-start.6
  220.1 2.1 reshape.40
  222.2 2.1 reshape.41
  224.4 0.0 collective-permute-done.10.r_ref
  224.4 2.3 add_chunk.5.refs_0_
  226.7 0.0 collective-permute-done.9.r_ref
  226.7 2.8 %add_chunk.6.refs_0_ = bf16[1024,2048]{1,0:T(8,128)(2,1)} custom-call(bf16[1024,2048]{1,0:T(8,128)(2,1)} %x_ref.11, bf16[256,2048]{1,0:T(8,128)(2,1)} %chunk_part.6.p_ref, bf16[256,2048]{1,0:T(8,128)(2,1)} %collective-permute-done.9.r_ref, bf16[1024,2048]{1,0:T(8,128)(2,1)} %add_chunk.5.refs_0_), custom_call_target="tpu_custom_call", output_to_operand_aliasing={{}: (3, {})} | custom-call | flops 2097152 | bytes 4194304 | tf_op jit(solution)/shard_map/add_chunk/pallas_call | solution.py:255
  229.5 0.0 collective-permute-done.8.r_ref
  229.5 2.8 %add_chunk.7.refs_0_ = bf16[1024,2048]{1,0:T(8,128)(2,1)} custom-call(bf16[1024,2048]{1,0:T(8,128)(2,1)} %x_ref.11, bf16[256,2048]{1,0:T(8,128)(2,1)} %chunk_part.7.p_ref, bf16[256,2048]{1,0:T(8,128)(2,1)} %collective-permute-done.8.r_ref, bf16[1024,2048]{1,0:T(8,128)(2,1)} %add_chunk.6.refs_0_), custom_call_target="tpu_custom_call", output_to_operand_aliasing={{}: (3, {})} | custom-call | flops 2097152 | bytes 4194304 | tf_op jit(solution)/shard_map/add_chunk/pallas_call | solution.py:255
  232.4 0.0 collective-permute-done.7.r_ref
  232.4 2.8 %add_chunk.8.refs_0_ = bf16[1024,2048]{1,0:T(8,128)(2,1)} custom-call(bf16[1024,2048]{1,0:T(8,128)(2,1)} %x_ref.11, bf16[256,2048]{1,0:T(8,128)(2,1)} %chunk_part.8.p_ref, bf16[256,2048]{1,0:T(8,128)(2,1)} %collective-permute-done.7.r_ref, bf16[1024,2048]{1,0:T(8,128)(2,1)} %add_chunk.7.refs_0_), custom_call_target="tpu_custom_call", output_to_operand_aliasing={{}: (3, {})} | custom-call | flops 2097152 | bytes 4194304 | tf_op jit(solution)/shard_map/add_chunk/pallas_call | solution.py:255
  235.2 0.0 collective-permute-done.6.r_ref
  235.2 2.3 add_chunk.9
  (2 shorter events, 0.0 us)
Async XLA Ops:
  10.0 52.2 %collective-permute-start.3 = (bf16[512,1024]{1,0:T(8,128)(2,1)}, bf16[512,1024]{1,0:T(8,128)(2,1)}, u32[]{:S(2)}, u32[]{:S(2)}) collective-permute-start(bf16[512,1024]{1,0:T(8,128)(2,1)} %get-tuple-element.31.v0), channel_id=1, source_target_pairs={{0,2},{1,3},{4,6},{5,7}} | collective-permute-start | bytes 3145736 | tf_op jit(solution)/shard_map/ppermute | solution.py:281
  11.3 74.6 %collective-permute-start.1 = (bf16[512,1024]{1,0:T(8,128)(2,1)}, bf16[512,1024]{1,0:T(8,128)(2,1)}, u32[]{:S(2)}, u32[]{:S(2)}) collective-permute-start(bf16[512,1024]{1,0:T(8,128)(2,1)} %get-tuple-element.31.v0), channel_id=1, source_target_pairs={{0,1},{2,3},{4,5},{6,7}} | collective-permute-start | bytes 3145736 | tf_op jit(solution)/shard_map/ppermute | solution.py:282
  23.7 35.0 %collective-permute-start.2 = (bf16[1024,512]{1,0:T(8,128)(2,1)}, bf16[1024,512]{1,0:T(8,128)(2,1)}, u32[]{:S(2)}, u32[]{:S(2)}) collective-permute-start(bf16[1024,512]{1,0:T(8,128)(2,1)} %shard_map.121.k0), channel_id=1, source_target_pairs={{0,2},{1,3},{4,6},{5,7}} | collective-permute-start | bytes 3145736 | tf_op jit(solution)/shard_map/ppermute | solution.py:281
  25.0 60.9 %collective-permute-start = (bf16[1024,512]{1,0:T(8,128)(2,1)}, bf16[1024,512]{1,0:T(8,128)(2,1)}, u32[]{:S(2)}, u32[]{:S(2)}) collective-permute-start(bf16[1024,512]{1,0:T(8,128)(2,1)} %shard_map.121.k0), channel_id=1, source_target_pairs={{0,1},{2,3},{4,5},{6,7}} | collective-permute-start | bytes 3145736 | tf_op jit(solution)/shard_map/ppermute | solution.py:282
  58.7 27.2 %collective-permute-start.4 = (bf16[1024,512]{1,0:T(8,128)(2,1)}, bf16[1024,512]{1,0:T(8,128)(2,1)}, u32[]{:S(2)}, u32[]{:S(2)}) collective-permute-start(bf16[1024,512]{1,0:T(8,128)(2,1)} %collective-permute-done.2.k2), channel_id=1, source_target_pairs={{2,3},{3,2},{6,7},{7,6}} | collective-permute-start | bytes 3145736 | tf_op jit(solution)/shard_map/ppermute | solution.py:283
  62.2 23.8 %collective-permute-start.5 = (bf16[512,1024]{1,0:T(8,128)(2,1)}, bf16[512,1024]{1,0:T(8,128)(2,1)}, u32[]{:S(2)}, u32[]{:S(2)}) collective-permute-start(bf16[512,1024]{1,0:T(8,128)(2,1)} %collective-permute-done.3.v2), channel_id=1, source_target_pairs={{2,3},{3,2},{6,7},{7,6}} | collective-permute-start | bytes 3145736 | tf_op jit(solution)/shard_map/ppermute | solution.py:283
  132.3 94.4 %collective-permute-start.9 = (bf16[256,2048]{1,0:T(8,128)(2,1)}, bf16[256,2048]{1,0:T(8,128)(2,1)}, u32[]{:S(2)}, u32[]{:S(2)}) collective-permute-start(bf16[256,2048]{1,0:T(8,128)(2,1)} %chunk_part.6.p_ref), channel_id=1, source_target_pairs={{0,4},{4,0},{1,5},{5,1},{2,6},{6,2},{3,7},{7,3}} | collective-permute-start | bytes 3145736 | tf_op jit(solution)/shard_map/ppermute | solution.py:307
  163.5 66.0 %collective-permute-start.8 = (bf16[256,2048]{1,0:T(8,128)(2,1)}, bf16[256,2048]{1,0:T(8,128)(2,1)}, u32[]{:S(2)}, u32[]{:S(2)}) collective-permute-start(bf16[256,2048]{1,0:T(8,128)(2,1)} %chunk_part.7.p_ref), channel_id=1, source_target_pairs={{0,4},{4,0},{1,5},{5,1},{2,6},{6,2},{3,7},{7,3}} | collective-permute-start | bytes 3145736 | tf_op jit(solution)/shard_map/ppermute | solution.py:307
  194.3 38.1 %collective-permute-start.7 = (bf16[256,2048]{1,0:T(8,128)(2,1)}, bf16[256,2048]{1,0:T(8,128)(2,1)}, u32[]{:S(2)}, u32[]{:S(2)}) collective-permute-start(bf16[256,2048]{1,0:T(8,128)(2,1)} %chunk_part.8.p_ref), channel_id=1, source_target_pairs={{0,4},{4,0},{1,5},{5,1},{2,6},{6,2},{3,7},{7,3}} | collective-permute-start | bytes 3145736 | tf_op jit(solution)/shard_map/ppermute | solution.py:307
  195.5 28.8 %collective-permute-start.10 = (bf16[128,2048]{1,0:T(8,128)(2,1)}, bf16[128,2048]{1,0:T(8,128)(2,1)}, u32[]{:S(2)}, u32[]{:S(2)}) collective-permute-start(bf16[128,2048]{1,0:T(8,128)(2,1)} %chunk_part.5.p_ref), channel_id=1, source_target_pairs={{0,4},{4,0},{1,5},{5,1},{2,6},{6,2},{3,7},{7,3}} | collective-permute-start | bytes 1572872 | tf_op jit(solution)/shard_map/ppermute | solution.py:307
  218.8 16.4 %collective-permute-start.6 = (bf16[128,2048]{1,0:T(8,128)(2,1)}, bf16[128,2048]{1,0:T(8,128)(2,1)}, u32[]{:S(2)}, u32[]{:S(2)}) collective-permute-start(bf16[128,2048]{1,0:T(8,128)(2,1)} %chunk_part.9.p_ref), channel_id=1, source_target_pairs={{0,4},{4,0},{1,5},{5,1},{2,6},{6,2},{3,7},{7,3}} | collective-permute-start | bytes 1572872 | tf_op jit(solution)/shard_map/ppermute | solution.py:307

commit v2 on v0

v2 whole, which is shorter than its diff:
```python
import functools
import math

import jax
import jax.numpy as jnp
from jax import lax
from jax.experimental import pallas as pl
from jax.experimental.pallas import tpu as pltpu
from jax.sharding import PartitionSpec as P

HEAD_DIM = 128
ROPE_BASE = 4000000
LN_EPS = 1e-5
F32 = jnp.float32
BF16 = jnp.bfloat16
MESH = pl.DeviceIdType.MESH
VMEM_LIMIT = 67043328

WBLK = 256
RING = 8
RBLK = 256
CHUNK = 128
KEYS = 512


def layer_kernel(x_hbm, gain_ref, cos_ref, sin_ref, wq_hbm, wk_hbm, wv_hbm, wo_hbm, wg_hbm, wu_hbm, wd_hbm,
                 out_hbm, k_hbm, v_hbm,
                 x_buf, h_buf, ring, act, q_buf, k_all, vt_all, v_own, wo, wd, recv, mlp, qs, o_buf, top_ref, sum_ref, acc_ref,
                 x_sem, ring_sem, wo_sem, wd_sem, kv_sem, out_sem,
                 cross_send, cross_recv, up_send, up_recv, relay_send, relay_recv, part_send, part_recv):
    me = lax.axis_index("cp")
    tp = lax.axis_index("tp")
    odd = me % 2
    partner = me + 1 - 2 * odd
    across = (me + 2) % 4
    rows, width = x_buf.shape
    kv_heads = k_all.shape[1] // HEAD_DIM
    n_rblk = rows // RBLK
    n_chunk = rows // CHUNK
    n_ff = act.shape[1] // WBLK
    part = h_buf

    def x_copy(b):
        r = pl.ds(pl.multiple_of(b * RBLK, RBLK), RBLK)
        return pltpu.make_async_copy(x_hbm.at[r, :], x_buf.at[r, :], x_sem.at[b])

    def w_copy(w_hbm, blk, slot):
        c = pl.ds(pl.multiple_of(blk * WBLK, WBLK), WBLK)
        return pltpu.make_async_copy(w_hbm.at[:, c], ring.at[slot], ring_sem.at[slot])

    wo_copy = pltpu.make_async_copy(wo_hbm, wo, wo_sem)
    wd_copy = pltpu.make_async_copy(wd_hbm, wd, wd_sem)

    x_copy(0).start()
    w_copy(wv_hbm, 0, 0).start()
    w_copy(wv_hbm, 1, 1).start()
    for b in range(1, n_rblk):
        x_copy(b).start()
    w_copy(wk_hbm, 0, 2).start()
    w_copy(wk_hbm, 1, 3).start()
    for j in range(4):
        w_copy(wq_hbm, j, 4 + j).start()

    barrier = pltpu.get_barrier_semaphore()
    pl.semaphore_signal(barrier, inc=1, device_id={"tp": 1 - tp}, device_id_type=MESH)
    pl.semaphore_signal(barrier, inc=1, device_id={"cp": partner}, device_id_type=MESH)
    pl.semaphore_signal(barrier, inc=1, device_id={"cp": across}, device_id_type=MESH)

    def region(owner, kind, b):
        at = pl.ds(pl.multiple_of(owner * rows + b * RBLK, RBLK), RBLK)
        return k_all.at[at, :] if kind else vt_all.at[:, at]

    def kv_copy(owner, kind, b, sends, recvs, target):
        ref = region(owner, kind, b)
        i = kind * n_rblk + b
        return pltpu.make_async_remote_copy(ref, ref, sends.at[i], recvs.at[i], device_id={"cp": target}, device_id_type=MESH)

    def cross(owner, kind, b):
        return kv_copy(owner, kind, b, cross_send, cross_recv, (owner + 2) % 4)

    def up(owner, kind, b):
        return kv_copy(owner, kind, b, up_send, up_recv, (owner + 1) % 4)

    def relay(owner, kind, b):
        return kv_copy(owner, kind, b, relay_send, relay_recv, 3 - owner)

    def send_piece(kind, b):
        @pl.when(me < 2)
        def _():
            cross(me, kind, b).start()

        @pl.when(odd == 0)
        def _():
            up(me, kind, b).start()

    def relay_piece(kind, b):
        owner = me - 2
        cross(owner, kind, b).wait_recv()
        kv_copy(owner, kind, b, relay_send, relay_recv, partner).start()

    def part_copy(c):
        r = pl.ds(pl.multiple_of(c * CHUNK, CHUNK), CHUNK)
        return pltpu.make_async_remote_copy(part.at[r, :], recv.at[r, :], part_send.at[c], part_recv.at[c],
                                            device_id={"tp": 1 - tp}, device_id_type=MESH)

    w_copy(wv_hbm, 0, 0).wait()
    w_copy(wv_hbm, 1, 1).wait()

    @pl.loop(0, n_rblk)
    def _(b):
        x_copy(b).wait()
        r = pl.ds(pl.multiple_of(b * RBLK, RBLK), RBLK)
        x = x_buf[r, :].astype(F32)
        mean = jnp.mean(x, axis=-1, keepdims=True)
        cent = x - mean
        var = jnp.mean(cent * cent, axis=-1, keepdims=True)
        h = (cent * lax.rsqrt(var + LN_EPS) * gain_ref[...].astype(F32)).astype(BF16)
        h_buf[r, :] = h
        for j in range(2):
            v = jnp.dot(h, ring[j], preferred_element_type=F32).astype(BF16)
            v_own[r, j * WBLK:(j + 1) * WBLK] = v
            at = pl.ds(pl.multiple_of(me * rows + b * RBLK, RBLK), RBLK)
            vt_all[j * WBLK:(j + 1) * WBLK, at] = v.T

        @pl.when(b == 0)
        def _():
            pl.semaphore_wait(barrier, 3)

        send_piece(0, b)

    v_out = pltpu.make_async_copy(v_own, v_hbm, kv_sem.at[0])
    v_out.start()

    lane = lax.broadcasted_iota(jnp.int32, (WBLK, WBLK), 0)
    other = lax.broadcasted_iota(jnp.int32, (WBLK, WBLK), 1)
    swap = jnp.where(lane == other + 1 - 2 * (other % 2), 1.0, 0.0).astype(BF16)

    def rope(r, w):
        proj = jnp.dot(h_buf[r, :], w, preferred_element_type=F32).astype(BF16)
        swapped = jnp.dot(proj, swap, preferred_element_type=F32)
        cos = cos_ref[r, :]
        sin = sin_ref[r, :]
        halves = []
        for i in range(WBLK // HEAD_DIM):
            c = slice(i * HEAD_DIM, (i + 1) * HEAD_DIM)
            halves.append((proj[:, c].astype(F32) * cos + swapped[:, c] * sin).astype(BF16))
        return jnp.concatenate(halves, axis=1)

    w_copy(wk_hbm, 0, 2).wait()
    w_copy(wk_hbm, 1, 3).wait()

    @pl.loop(0, n_rblk)
    def _(b):
        r = pl.ds(pl.multiple_of(b * RBLK, RBLK), RBLK)
        at = pl.ds(pl.multiple_of(me * rows + b * RBLK, RBLK), RBLK)
        for j in range(2):
            k_all[at, j * WBLK:(j + 1) * WBLK] = rope(r, ring[2 + j])
        send_piece(1, b)

    k_out = pltpu.make_async_copy(k_all.at[pl.ds(pl.multiple_of(me * rows, RBLK), rows), :], k_hbm, kv_sem.at[1])
    k_out.start()

    def ff_copies(s):
        slot = 2 * (s % 4)
        return w_copy(wg_hbm, s, slot), w_copy(wu_hbm, s, slot + 1)

    for s in range(2):
        for copy in ff_copies(s):
            copy.start()

    @pl.loop(0, 4)
    def _(j):
        w_copy(wq_hbm, j, 4 + j).wait()
        for b in range(n_rblk):
            r = slice(b * RBLK, (b + 1) * RBLK)
            q_buf[r, pl.ds(pl.multiple_of(j * WBLK, WBLK), WBLK)] = rope(r, ring[4 + j])

    for s in range(2, 4):
        for copy in ff_copies(s):
            copy.start()
    wo_copy.start()
    wd_copy.start()

    @pl.loop(0, n_ff)
    def _(s):
        for copy in ff_copies(s):
            copy.wait()
        slot = 2 * (s % 4)
        for b in range(n_rblk):
            r = slice(b * RBLK, (b + 1) * RBLK)
            h = h_buf[r, :]
            gate = jnp.dot(h, ring[slot], preferred_element_type=F32).astype(BF16).astype(F32)
            up_ = jnp.dot(h, ring[slot + 1], preferred_element_type=F32).astype(BF16).astype(F32)
            act[r, pl.ds(pl.multiple_of(s * WBLK, WBLK), WBLK)] = (jax.nn.silu(gate) * up_).astype(BF16)

        @pl.when(s + 4 < n_ff)
        def _():
            for copy in ff_copies(s + 4):
                copy.start()

        @pl.when((me >= 2) & (s >= 2) & (s < 6))
        def _():
            relay_piece(0, s - 2)

        @pl.when((me >= 2) & (s >= 7) & (s % 2 == 1))
        def _():
            relay_piece(1, (s - 7) // 2)

    def down(c):
        r = pl.ds(pl.multiple_of(c * CHUNK, CHUNK), CHUNK)
        a = act[r, :]
        for j in range(4):
            cols = slice(j * (width // 4), (j + 1) * (width // 4))
            mlp[:, cols] = jnp.dot(a, wd[:, cols], preferred_element_type=F32)

    wo_copy.wait()
    wd_copy.wait()
    down(0)

    @pl.when(me >= 2)
    def _():
        relay_piece(1, 3)
        for kind in range(2):
            for b in range(n_rblk):
                kv_copy(3 - me, kind, b, relay_send, relay_recv, partner).wait_recv()

    @pl.when(odd == 1)
    def _():
        for kind in range(2):
            for b in range(n_rblk):
                up(me - 1, kind, b).wait_recv()

    scale = HEAD_DIM ** -0.5 * math.log2(math.e)

    def attend(j, first):
        at = pl.ds(pl.multiple_of(j * KEYS, KEYS), KEYS)
        for g in range(kv_heads):
            heads = slice(g * HEAD_DIM, (g + 1) * HEAD_DIM)
            s = lax.dot_general(k_all[at, heads], qs[g], (((1,), (1,)), ((), ())), preferred_element_type=F32) * scale
            if first is not None:
                key_id = lax.broadcasted_iota(jnp.int32, s.shape, 0)
                query_id = lax.broadcasted_iota(jnp.int32, s.shape, 1) % CHUNK
                s = jnp.where(key_id <= query_id + first, s, -jnp.inf)
            old = top_ref[g]
            new = jnp.maximum(old, jnp.max(s, axis=0, keepdims=True))
            factor = jnp.exp2(old - new)
            weight = jnp.exp2(s - new)
            top_ref[g] = new
            sum_ref[g] = sum_ref[g] * factor + jnp.sum(weight, axis=0, keepdims=True)
            acc_ref[g] = acc_ref[g] * factor + jnp.dot(vt_all[heads, at], weight.astype(BF16), preferred_element_type=F32)

    @pl.loop(0, n_chunk)
    def _(c):
        r = pl.ds(pl.multiple_of(c * CHUNK, CHUNK), CHUNK)
        for g in range(kv_heads):
            for i in range(2):
                col = (2 * g + i) * HEAD_DIM
                qs[g, i * CHUNK:(i + 1) * CHUNK, :] = q_buf[r, col:col + HEAD_DIM]
        top_ref[...] = jnp.full_like(top_ref, -jnp.inf)
        sum_ref[...] = jnp.zeros_like(sum_ref)
        acc_ref[...] = jnp.zeros_like(acc_ref)
        full = me * (rows // KEYS) + c // (KEYS // CHUNK)

        @pl.loop(0, full)
        def _(j):
            attend(j, None)

        attend(full, (c % (KEYS // CHUNK)) * CHUNK)
        for g in range(kv_heads):
            o = (acc_ref[g] / sum_ref[g]).T.astype(BF16)
            for i in range(2):
                col = (2 * g + i) * HEAD_DIM
                o_buf[:, col:col + HEAD_DIM] = o[i * CHUNK:(i + 1) * CHUNK, :]
        o = o_buf[...]
        for j in range(4):
            cols = slice(j * (width // 4), (j + 1) * (width // 4))
            part[r, cols] = (jnp.dot(o, wo[:, cols], preferred_element_type=F32) + mlp[:, cols]).astype(BF16)
        part_copy(c).start()

        @pl.when(c + 1 < n_chunk)
        def _():
            down(c + 1)

    def out_copy(c):
        r = pl.ds(pl.multiple_of(c * CHUNK, CHUNK), CHUNK)
        return pltpu.make_async_copy(x_buf.at[r, :], out_hbm.at[r, :], out_sem.at[c])

    @pl.loop(0, n_chunk)
    def _(c):
        r = pl.ds(pl.multiple_of(c * CHUNK, CHUNK), CHUNK)
        part_copy(c).wait_recv()
        x_buf[r, :] = (x_buf[r, :].astype(F32) + (part[r, :].astype(F32) + recv[r, :].astype(F32))).astype(BF16)
        out_copy(c).start()

    @pl.loop(0, n_chunk)
    def _(c):
        out_copy(c).wait()
        part_copy(c).wait_send()

    v_out.wait()
    k_out.wait()
    for kind in range(2):
        for b in range(n_rblk):
            @pl.when(me < 2)
            def _():
                cross(me, kind, b).wait_send()

            @pl.when(odd == 0)
            def _():
                up(me, kind, b).wait_send()

            @pl.when(me >= 2)
            def _():
                kv_copy(me - 2, kind, b, relay_send, relay_recv, partner).wait_send()


def rope_tables(positions):
    lane = jnp.arange(HEAD_DIM)
    exponent = (lane - lane % 2).astype(F32) / HEAD_DIM
    inv_freq = 1.0 / (ROPE_BASE ** exponent)
    angles = positions.astype(F32)[:, None] * inv_freq[None, :]
    sign = jnp.where(lane % 2 == 0, -1.0, 1.0).astype(F32)
    return jnp.cos(angles), jnp.sin(angles) * sign[None, :]


def solution(mesh):
    n_cp = mesh.shape['cp']

    def local_layer(hidden, positions, ln_gain, w_q, w_k, w_v, w_o, w_gate, w_up, w_down):
        rows, width = hidden.shape
        q_cols = w_q.shape[1]
        kv_cols = w_k.shape[1]
        ff = w_gate.shape[1]
        kv_heads = kv_cols // HEAD_DIM
        keys = n_cp * rows
        n_chunk = rows // CHUNK
        pieces = 2 * (rows // RBLK)
        cos, sin = rope_tables(positions)
        hbm = pl.BlockSpec(memory_space=pl.ANY)
        vmem = pl.BlockSpec(memory_space=pltpu.VMEM)
        dma = pltpu.SemaphoreType.DMA
        out, k, v = pl.pallas_call(
            layer_kernel,
            in_specs=[hbm, vmem, vmem, vmem] + [hbm] * 7,
            out_specs=[hbm] * 3,
            out_shape=[
                jax.ShapeDtypeStruct((rows, width), BF16),
                jax.ShapeDtypeStruct((rows, kv_cols), BF16),
                jax.ShapeDtypeStruct((rows, kv_cols), BF16),
            ],
            scratch_shapes=[
                pltpu.VMEM((rows, width), BF16),
                pltpu.VMEM((rows, width), BF16),
                pltpu.VMEM((RING, width, WBLK), BF16),
                pltpu.VMEM((rows, ff), BF16),
                pltpu.VMEM((rows, q_cols), BF16),
                pltpu.VMEM((keys, kv_cols), BF16),
                pltpu.VMEM((kv_cols, keys), BF16),
                pltpu.VMEM((rows, kv_cols), BF16),
                pltpu.VMEM((q_cols, width), BF16),
                pltpu.VMEM((ff, width), BF16),
                pltpu.VMEM((rows, width), BF16),
                pltpu.VMEM((CHUNK, width), F32),
                pltpu.VMEM((kv_heads, 2 * CHUNK, HEAD_DIM), BF16),
                pltpu.VMEM((CHUNK, q_cols), BF16),
                pltpu.VMEM((kv_heads, 1, 2 * CHUNK), F32),
                pltpu.VMEM((kv_heads, 1, 2 * CHUNK), F32),
                pltpu.VMEM((kv_heads, HEAD_DIM, 2 * CHUNK), F32),
                dma((rows // RBLK,)), dma((RING,)), dma, dma, dma((2,)), dma((n_chunk,)),
                dma((pieces,)), dma((pieces,)), dma((pieces,)), dma((pieces,)), dma((pieces,)), dma((pieces,)),
                dma((n_chunk,)), dma((n_chunk,)),
            ],
            compiler_params=pltpu.CompilerParams(collective_id=0, has_side_effects=True, vmem_limit_bytes=VMEM_LIMIT),
            name="layer",
        )(hidden, ln_gain.reshape(1, width), cos, sin, w_q, w_k, w_v, w_o, w_gate, w_up, w_down)
        shape = (rows, kv_heads, HEAD_DIM)
        return out, k.reshape(shape), v.reshape(shape)

    row_spec = P(('dp', 'cp'), None)
    col_spec = P(None, 'tp')
    cache_spec = P(('dp', 'cp'), 'tp', None)
    in_specs = (row_spec, P(('dp', 'cp')), P(None), col_spec, col_spec, col_spec, P('tp', None), col_spec, col_spec, P('tp', None))
    return jax.shard_map(local_layer, mesh=mesh, in_specs=in_specs, out_specs=(row_spec, cache_spec, cache_spec), check_vma=False)
```

time: 546 us -> 204 us (0.37)
  the two profiles are of different devices: /device:TPU:0 before, /device:TPU:3 now
where the time goes in v2:
time: 204 us
  Pallas kernels  189 us (93%)
  local copies, waits for them, and re-layouts  10.3 us (5%)
  other arithmetic  3.74 us (2%)
    pallas_call x1, Pallas kernels, local_layer(): pl.pallas_call(layer_kernel, in_specs=[hbm, vmem, vmem, vmem] + [hbm] * 7...  189 us
    unnamed x1, local copies, waits for them, and re-layouts  4.79 us
    reshape x2, local copies, waits for them, and re-layouts, local_layer(): return (out, k.reshape(shape), v.reshape(shape))  4.27 us

profile of v2, /device:TPU:3, one launch (start us, length us, event | category | flops | bytes accessed | tf_op | source)
XLA Modules:
  0.0 203.9 jit_solution(1468503162137235895)
XLA Ops:
  0.6 0.7 convert_element_type.10
  1.3 1.3 reshape.35.gain_ref
  2.6 3.0 %fusion = (f32[1024,128]{1,0:T(8,128)}, f32[1024,128]{1,0:T(8,128)}) fusion(f32[128]{0:T(128)S(1)} %get-tuple-element.11, f32[128]{0:T(128)S(1)} %get-tuple-element.12, f32[1024]{0:T(1024)S(1)} %convert_element_type.10), kind=kLoop, calls=%fused_computation.2 | loop fusion | flops 262144 | bytes 1053696 | tf_op jit(solution)/shard_map/mul | solution.py:323
  5.7 189.2 %layer.1 = (bf16[1024,2048]{1,0:T(8,128)(2,1)}, bf16[1024,512]{1,0:T(8,128)(2,1)}, bf16[1024,512]{1,0:T(8,128)(2,1)}) custom-call(bf16[1024,2048]{1,0:T(8,128)(2,1)} %x_hbm.1, bf16[1,2048]{1,0:T(2,128)(2,1)} %reshape.35.gain_ref, f32[1024,128]{1,0:T(8,128)} %get-tuple-element.10.cos_ref, f32[1024,128]{1,0:T(8,128)} %get-tuple-element.9.sin_ref, ...), custom_call_target="tpu_custom_call" | custom-call | tf_op jit(solution)/shard_map/layer/pallas_call | solution.py:342
  194.8 2.1 %reshape.36 = bf16[1024,4,128]{2,1,0:T(4,128)(2,1)} reshape(bf16[1024,512]{1,0:T(8,128)(2,1)} %get-tuple-element.7) | data formatting | bytes 2097152 | tf_op jit(solution)/shard_map/reshape | solution.py:377
  197.0 2.1 %reshape.37 = bf16[1024,4,128]{2,1,0:T(4,128)(2,1)} reshape(bf16[1024,512]{1,0:T(8,128)(2,1)} %get-tuple-element.8) | data formatting | bytes 2097152 | tf_op jit(solution)/shard_map/reshape | solution.py:377
  199.1 4.8 %copy.14 = bf16[1024,2048]{1,0:T(8,128)(2,1)} copy(bf16[1024,2048]{1,0:T(8,128)(2,1)} %get-tuple-element.16) | data formatting | bytes 8388608
  (1 shorter events, 0.0 us)

commit v3 on v2

v3 whole, which is shorter than its diff:
```python
import functools
import math

import jax
import jax.numpy as jnp
from jax import lax
from jax.experimental import pallas as pl
from jax.experimental.pallas import tpu as pltpu
from jax.sharding import PartitionSpec as P

HEAD_DIM = 128
ROPE_BASE = 4000000
LN_EPS = 1e-5
F32 = jnp.float32
BF16 = jnp.bfloat16
MESH = pl.DeviceIdType.MESH
VMEM_LIMIT = 67043328

WBLK = 256
RING = 8
RBLK = 256
CHUNK = 128
KEYS = 512
VIA = 1
VIA_AFTER = 5
VIA_PIECES = 4


def layer_kernel(x_hbm, gain_ref, cos_ref, sin_ref, wq_hbm, wk_hbm, wv_hbm, wo_hbm, wg_hbm, wu_hbm, wd_hbm,
                 out_hbm, k_hbm, v_hbm,
                 x_buf, h_buf, ring, act, q_buf, k_all, vt_all, v_own, wo, wd, recv, mlp, qs, o_buf, s_ref, blk_ref, top_ref, sum_ref, acc_ref,
                 x_sem, ring_sem, wo_sem, wd_sem, kv_sem, out_sem,
                 cross_send, cross_recv, up_send, up_recv, relay_send, relay_recv, part_send, part_recv, via, via_send, via_recv):
    me = lax.axis_index("cp")
    tp = lax.axis_index("tp")
    odd = me % 2
    partner = me + 1 - 2 * odd
    across = (me + 2) % 4
    rows, width = x_buf.shape
    kv_heads = k_all.shape[1] // HEAD_DIM
    n_rblk = rows // RBLK
    n_chunk = rows // CHUNK
    n_ff = act.shape[1] // WBLK
    part = h_buf

    def x_copy(b):
        r = pl.ds(pl.multiple_of(b * RBLK, RBLK), RBLK)
        return pltpu.make_async_copy(x_hbm.at[r, :], x_buf.at[r, :], x_sem.at[b])

    def w_copy(w_hbm, blk, slot):
        c = pl.ds(pl.multiple_of(blk * WBLK, WBLK), WBLK)
        return pltpu.make_async_copy(w_hbm.at[:, c], ring.at[slot], ring_sem.at[slot])

    wo_copy = pltpu.make_async_copy(wo_hbm, wo, wo_sem)
    wd_copy = pltpu.make_async_copy(wd_hbm, wd, wd_sem)

    x_copy(0).start()
    w_copy(wv_hbm, 0, 0).start()
    w_copy(wv_hbm, 1, 1).start()
    for b in range(1, n_rblk):
        x_copy(b).start()
    w_copy(wk_hbm, 0, 2).start()
    w_copy(wk_hbm, 1, 3).start()
    for j in range(4):
        w_copy(wq_hbm, j, 4 + j).start()
    wo_copy.start()
    wd_copy.start()

    barrier = pltpu.get_barrier_semaphore()
    pl.semaphore_signal(barrier, inc=1, device_id={"tp": 1 - tp}, device_id_type=MESH)
    pl.semaphore_signal(barrier, inc=1, device_id={"cp": partner}, device_id_type=MESH)
    pl.semaphore_signal(barrier, inc=1, device_id={"cp": across}, device_id_type=MESH)

    def region(owner, kind, b):
        if kind:
            at = pl.ds(pl.multiple_of(owner * rows + (b % 2) * (rows // 2), RBLK), rows // 2)
            return k_all.at[at, pl.ds(pl.multiple_of((b // 2) * WBLK, WBLK), WBLK)]
        return vt_all.at[:, pl.ds(pl.multiple_of(owner * rows + b * RBLK, RBLK), RBLK)]

    def kv_copy(owner, kind, b, sends, recvs, target):
        ref = region(owner, kind, b)
        i = kind * n_rblk + b
        return pltpu.make_async_remote_copy(ref, ref, sends.at[i], recvs.at[i], device_id={"cp": target}, device_id_type=MESH)

    def cross(owner, kind, b):
        return kv_copy(owner, kind, b, cross_send, cross_recv, (owner + 2) % 4)

    def up(owner, kind, b):
        return kv_copy(owner, kind, b, up_send, up_recv, (owner + 1) % 4)

    def relay(owner, kind, b):
        return kv_copy(owner, kind, b, relay_send, relay_recv, 3 - owner)

    def send_piece(kind, b):
        @pl.when(me < 2)
        def _():
            cross(me, kind, b).start()

        @pl.when(odd == 0)
        def _():
            up(me, kind, b).start()

    def relay_piece(kind, b):
        owner = me - 2
        cross(owner, kind, b).wait_recv()
        kv_copy(owner, kind, b, relay_send, relay_recv, partner).start()

    def part_copy(c):
        r = pl.ds(pl.multiple_of(c * CHUNK, CHUNK), CHUNK)
        return pltpu.make_async_remote_copy(part.at[r, :], recv.at[r, :], part_send.at[c], part_recv.at[c],
                                            device_id={"tp": 1 - tp}, device_id_type=MESH)

    def via_copy(leg, i):
        n = CHUNK // VIA_PIECES
        rows_i = slice(i * n, (i + 1) * n)
        at = slice(VIA * CHUNK + i * n, VIA * CHUNK + (i + 1) * n)
        src = (part.at[at, :], via.at[0, rows_i, :], via.at[1, rows_i, :])[leg]
        dst = (via.at[0, rows_i, :], via.at[1, rows_i, :], recv.at[at, :])[leg]
        target = {"tp": 1 - tp} if leg == 1 else {"cp": across}
        return pltpu.make_async_remote_copy(src, dst, via_send.at[leg * VIA_PIECES + i], via_recv.at[leg * VIA_PIECES + i],
                                            device_id=target, device_id_type=MESH)

    gain = jnp.concatenate([gain_ref[i:i + 1, :] for i in range(width // HEAD_DIM)], axis=1).astype(F32)

    def norm(b):
        r = pl.ds(pl.multiple_of(b * RBLK, RBLK), RBLK)
        x = x_buf[r, :].astype(F32)
        mean = jnp.mean(x, axis=-1, keepdims=True)
        cent = x - mean
        var = jnp.mean(cent * cent, axis=-1, keepdims=True)
        h_buf[r, :] = (cent * lax.rsqrt(var + LN_EPS) * gain).astype(BF16)

    def project_v(b):
        r = pl.ds(pl.multiple_of(b * RBLK, RBLK), RBLK)
        at = pl.ds(pl.multiple_of(me * rows + b * RBLK, RBLK), RBLK)
        h = h_buf[r, :]
        for j in range(2):
            v = jnp.dot(h, ring[j], preferred_element_type=F32).astype(BF16)
            v_own[r, j * WBLK:(j + 1) * WBLK] = v
            vt_all[j * WBLK:(j + 1) * WBLK, at] = v.T

    x_copy(0).wait()
    norm(0)
    w_copy(wv_hbm, 0, 0).wait()
    w_copy(wv_hbm, 1, 1).wait()
    pl.semaphore_wait(barrier, 3)

    @pl.loop(0, n_rblk - 1)
    def _(b):
        x_copy(b + 1).wait()
        project_v(b)
        norm(b + 1)
        send_piece(0, b)

    project_v(n_rblk - 1)
    send_piece(0, n_rblk - 1)
    v_out = pltpu.make_async_copy(v_own, v_hbm, kv_sem.at[0])
    v_out.start()

    lane = lax.broadcasted_iota(jnp.int32, (WBLK, WBLK), 0)
    other = lax.broadcasted_iota(jnp.int32, (WBLK, WBLK), 1)
    swap = jnp.where(lane == other + 1 - 2 * (other % 2), 1.0, 0.0).astype(BF16)

    def rope_block(slot, dst, row0, col):
        proj = [None] * n_rblk

        def project(b):
            proj[b] = jnp.dot(h_buf[b * RBLK:(b + 1) * RBLK, :], ring[slot], preferred_element_type=F32).astype(BF16)

        project(0)
        for b in range(n_rblk):
            if b + 1 < n_rblk:
                project(b + 1)
            r = slice(b * RBLK, (b + 1) * RBLK)
            swapped = jnp.dot(proj[b], swap, preferred_element_type=F32)
            cos = cos_ref[r, :]
            sin = sin_ref[r, :]
            halves = []
            for i in range(WBLK // HEAD_DIM):
                c = slice(i * HEAD_DIM, (i + 1) * HEAD_DIM)
                halves.append((proj[b][:, c].astype(F32) * cos + swapped[:, c] * sin).astype(BF16))
            at = pl.ds(pl.multiple_of(row0 + b * RBLK, RBLK), RBLK)
            dst[at, pl.ds(pl.multiple_of(col, WBLK), WBLK)] = jnp.concatenate(halves, axis=1)

    @pl.loop(0, 2)
    def _(j):
        w_copy(wk_hbm, j, 2 + j).wait()
        rope_block(2 + j, k_all, me * rows, j * WBLK)
        send_piece(1, 2 * j)
        send_piece(1, 2 * j + 1)

    k_out = pltpu.make_async_copy(k_all.at[pl.ds(pl.multiple_of(me * rows, RBLK), rows), :], k_hbm, kv_sem.at[1])
    k_out.start()

    def ff_copies(s):
        slot = 2 * (s % 4)
        return w_copy(wg_hbm, s % n_ff, slot), w_copy(wu_hbm, s % n_ff, slot + 1)

    for s in range(2):
        for copy in ff_copies(s):
            copy.start()

    @pl.loop(0, 4)
    def _(j):
        w_copy(wq_hbm, j, 4 + j).wait()
        rope_block(4 + j, q_buf, 0, j * WBLK)

    for s in range(2, 4):
        for copy in ff_copies(s):
            copy.start()

    relay_steps = ((0, 0, 0), (2, 0, 1), (6, 0, 2), (10, 0, 3), (15, 1, 0), (19, 1, 1), (23, 1, 2))

    def feed(half):
        @pl.loop(half * n_ff, (half + 1) * n_ff)
        def _(s):
            for copy in ff_copies(s):
                copy.wait()
            slot = 2 * (s % 4)
            for b in range(half * n_rblk // 2, (half + 1) * n_rblk // 2):
                r = slice(b * RBLK, (b + 1) * RBLK)
                h = h_buf[r, :]
                gate = jnp.dot(h, ring[slot], preferred_element_type=F32).astype(BF16).astype(F32)
                up_ = jnp.dot(h, ring[slot + 1], preferred_element_type=F32).astype(BF16).astype(F32)
                act[r, pl.ds(pl.multiple_of((s % n_ff) * WBLK, WBLK), WBLK)] = (jax.nn.silu(gate) * up_).astype(BF16)

            @pl.when(s + 4 < 2 * n_ff)
            def _():
                for copy in ff_copies(s + 4):
                    copy.start()

            for step, kind, b in relay_steps:
                if half * n_ff <= step < (half + 1) * n_ff:
                    @pl.when((me >= 2) & (s == step))
                    def _():
                        relay_piece(kind, b)

    def down(c):
        r = pl.ds(pl.multiple_of(c * CHUNK, CHUNK), CHUNK)
        a = act[r, :]
        for j in range(4):
            cols = slice(j * (width // 4), (j + 1) * (width // 4))
            mlp[:, cols] = jnp.dot(a, wd[:, cols], preferred_element_type=F32)

    scale = HEAD_DIM ** -0.5 * math.log2(math.e)

    def head(g):
        return slice(g * HEAD_DIM, (g + 1) * HEAD_DIM)

    def key_rows(j):
        return pl.ds(pl.multiple_of(j * KEYS, KEYS), KEYS)

    def score(j, g):
        s = lax.dot_general(k_all[key_rows(j), head(g)], qs[g], (((1,), (1,)), ((), ())), preferred_element_type=F32)
        s_ref[g] = s
        blk_ref[g] = jnp.max(s, axis=0, keepdims=True)

    def weigh(g, s, block_top):
        old = top_ref[g]
        new = jnp.maximum(old, block_top)
        factor = jnp.exp2((old - new) * scale)
        weight = jnp.exp2((s - new) * scale)
        top_ref[g] = new
        sum_ref[g] = sum_ref[g] * factor + jnp.sum(weight, axis=0, keepdims=True)
        return factor, weight.astype(BF16)

    def collect(j, g, factor, weight):
        acc_ref[g] = acc_ref[g] * factor + jnp.dot(vt_all[head(g), key_rows(j)], weight, preferred_element_type=F32)

    def chunk(c, stop):
        r = pl.ds(pl.multiple_of(c * CHUNK, CHUNK), CHUNK)
        for g in range(kv_heads):
            for i in range(2):
                col = (2 * g + i) * HEAD_DIM
                qs[g, i * CHUNK:(i + 1) * CHUNK, :] = q_buf[r, col:col + HEAD_DIM]
        top_ref[...] = jnp.full_like(top_ref, -jnp.inf)
        sum_ref[...] = jnp.zeros_like(sum_ref)
        acc_ref[...] = jnp.zeros_like(acc_ref)
        full = me * (rows // KEYS) + c // (KEYS // CHUNK)
        for g in range(kv_heads):
            score(0, g)

        @pl.loop(0, full)
        def _(j):
            for g in range(kv_heads):
                factor, weight = weigh(g, s_ref[g], blk_ref[g])
                score(j + 1, g)
                collect(j, g, factor, weight)

        first = (c % (KEYS // CHUNK)) * CHUNK
        key_id = lax.broadcasted_iota(jnp.int32, (KEYS, 2 * CHUNK), 0)
        query_id = lax.broadcasted_iota(jnp.int32, (KEYS, 2 * CHUNK), 1) % CHUNK
        for g in range(kv_heads):
            s = jnp.where(key_id <= query_id + first, s_ref[g], -jnp.inf)
            factor, weight = weigh(g, s, jnp.max(s, axis=0, keepdims=True))
            collect(full, g, factor, weight)
        for g in range(kv_heads):
            o = (acc_ref[g] / sum_ref[g]).T.astype(BF16)
            for i in range(2):
                col = (2 * g + i) * HEAD_DIM
                o_buf[:, col:col + HEAD_DIM] = o[i * CHUNK:(i + 1) * CHUNK, :]
        o = o_buf[...]
        for j in range(4):
            cols = slice(j * (width // 4), (j + 1) * (width // 4))
            part[r, cols] = (jnp.dot(o, wo[:, cols], preferred_element_type=F32) + mlp[:, cols]).astype(BF16)

        @pl.when((me < 2) | (c != VIA))
        def _():
            part_copy(c).start()

        @pl.when((me >= 2) & (c == VIA))
        def _():
            for i in range(VIA_PIECES):
                via_copy(0, i).start()

        @pl.when((me < 2) & (c == VIA_AFTER))
        def _():
            for i in range(VIA_PIECES):
                via_copy(0, i).wait_recv()
                via_copy(1, i).start()

        @pl.when(c + 1 < stop)
        def _():
            down(c + 1)

    early = jnp.where(me < 2, n_chunk // 2, 0)
    feed(0)
    wo_copy.wait()
    wd_copy.wait()

    @pl.when(odd == 1)
    def _():
        for kind in range(2):
            for b in range(n_rblk):
                up(me - 1, kind, b).wait_recv()

    @pl.when(me < 2)
    def _():
        down(0)

    @pl.loop(0, early)
    def _(c):
        chunk(c, early)

    feed(1)
    down(early)

    @pl.when(me >= 2)
    def _():
        relay_piece(1, 3)
        for kind in range(2):
            for b in range(n_rblk):
                kv_copy(3 - me, kind, b, relay_send, relay_recv, partner).wait_recv()

    @pl.loop(early, n_chunk)
    def _(c):
        chunk(c, n_chunk)

    def out_copy(c):
        r = pl.ds(pl.multiple_of(c * CHUNK, CHUNK), CHUNK)
        return pltpu.make_async_copy(x_buf.at[r, :], out_hbm.at[r, :], out_sem.at[c])

    def finish(c):
        r = pl.ds(pl.multiple_of(c * CHUNK, CHUNK), CHUNK)
        x_buf[r, :] = (x_buf[r, :].astype(F32) + (part[r, :].astype(F32) + recv[r, :].astype(F32))).astype(BF16)
        out_copy(c).start()

    @pl.loop(0, n_chunk)
    def _(c):
        @pl.when((me < 2) & (c == VIA_AFTER + 1))
        def _():
            for i in range(VIA_PIECES):
                via_copy(1, i).wait_recv()
                via_copy(2, i).start()

        @pl.when((me >= 2) & (c == n_chunk - 1))
        def _():
            for i in range(VIA_PIECES):
                via_copy(2, i).wait_recv()
            finish(VIA)

        @pl.when((me < 2) | (c != VIA))
        def _():
            part_copy(c).wait_recv()
            finish(c)

    @pl.loop(0, n_chunk)
    def _(c):
        out_copy(c).wait()

        @pl.when((me < 2) | (c != VIA))
        def _():
            part_copy(c).wait_send()

    for i in range(VIA_PIECES):
        @pl.when(me >= 2)
        def _():
            via_copy(0, i).wait_send()

        @pl.when(me < 2)
        def _():
            via_copy(1, i).wait_send()
            via_copy(2, i).wait_send()

    v_out.wait()
    k_out.wait()
    for kind in range(2):
        for b in range(n_rblk):
            @pl.when(me < 2)
            def _():
                cross(me, kind, b).wait_send()

            @pl.when(odd == 0)
            def _():
                up(me, kind, b).wait_send()

            @pl.when(me >= 2)
            def _():
                kv_copy(me - 2, kind, b, relay_send, relay_recv, partner).wait_send()


def rope_tables(positions):
    lane = jnp.arange(HEAD_DIM)
    exponent = (lane - lane % 2).astype(F32) / HEAD_DIM
    inv_freq = 1.0 / (ROPE_BASE ** exponent)
    angles = positions.astype(F32)[:, None] * inv_freq[None, :]
    sign = jnp.where(lane % 2 == 0, -1.0, 1.0).astype(F32)
    return jnp.cos(angles), jnp.sin(angles) * sign[None, :]


def solution(mesh):
    n_cp = mesh.shape['cp']

    def local_layer(hidden, positions, ln_gain, w_q, w_k, w_v, w_o, w_gate, w_up, w_down):
        rows, width = hidden.shape
        q_cols = w_q.shape[1]
        kv_cols = w_k.shape[1]
        ff = w_gate.shape[1]
        kv_heads = kv_cols // HEAD_DIM
        keys = n_cp * rows
        n_chunk = rows // CHUNK
        pieces = 2 * (rows // RBLK)
        cos, sin = rope_tables(positions)
        hbm = pl.BlockSpec(memory_space=pl.ANY)
        vmem = pl.BlockSpec(memory_space=pltpu.VMEM)
        dma = pltpu.SemaphoreType.DMA
        out, k, v = pl.pallas_call(
            layer_kernel,
            in_specs=[hbm, vmem, vmem, vmem] + [hbm] * 7,
            out_specs=[hbm] * 3,
            out_shape=[
                jax.ShapeDtypeStruct((rows, width), BF16),
                jax.ShapeDtypeStruct((rows, kv_cols), BF16),
                jax.ShapeDtypeStruct((rows, kv_cols), BF16),
            ],
            scratch_shapes=[
                pltpu.VMEM((rows, width), BF16),
                pltpu.VMEM((rows, width), BF16),
                pltpu.VMEM((RING, width, WBLK), BF16),
                pltpu.VMEM((rows, ff), BF16),
                pltpu.VMEM((rows, q_cols), BF16),
                pltpu.VMEM((keys, kv_cols), BF16),
                pltpu.VMEM((kv_cols, keys), BF16),
                pltpu.VMEM((rows, kv_cols), BF16),
                pltpu.VMEM((q_cols, width), BF16),
                pltpu.VMEM((ff, width), BF16),
                pltpu.VMEM((rows, width), BF16),
                pltpu.VMEM((CHUNK, width), F32),
                pltpu.VMEM((kv_heads, 2 * CHUNK, HEAD_DIM), BF16),
                pltpu.VMEM((CHUNK, q_cols), BF16),
                pltpu.VMEM((kv_heads, KEYS, 2 * CHUNK), F32),
                pltpu.VMEM((kv_heads, 1, 2 * CHUNK), F32),
                pltpu.VMEM((kv_heads, 1, 2 * CHUNK), F32),
                pltpu.VMEM((kv_heads, 1, 2 * CHUNK), F32),
                pltpu.VMEM((kv_heads, HEAD_DIM, 2 * CHUNK), F32),
                dma((rows // RBLK,)), dma((RING,)), dma, dma, dma((2,)), dma((n_chunk,)),
                dma((pieces,)), dma((pieces,)), dma((pieces,)), dma((pieces,)), dma((pieces,)), dma((pieces,)),
                dma((n_chunk,)), dma((n_chunk,)),
                pltpu.VMEM((2, CHUNK, width), BF16), dma((3 * VIA_PIECES,)), dma((3 * VIA_PIECES,)),
            ],
            compiler_params=pltpu.CompilerParams(collective_id=0, has_side_effects=True, vmem_limit_bytes=VMEM_LIMIT),
            name="layer",
        )(hidden, ln_gain.reshape(width // HEAD_DIM, HEAD_DIM), cos, sin, w_q, w_k, w_v, w_o, w_gate, w_up, w_down)
        shape = (rows, kv_heads, HEAD_DIM)
        return out, k.reshape(shape), v.reshape(shape)

    row_spec = P(('dp', 'cp'), None)
    col_spec = P(None, 'tp')
    cache_spec = P(('dp', 'cp'), 'tp', None)
    in_specs = (row_spec, P(('dp', 'cp')), P(None), col_spec, col_spec, col_spec, P('tp', None), col_spec, col_spec, P('tp', None))
    return jax.shard_map(local_layer, mesh=mesh, in_specs=in_specs, out_specs=(row_spec, cache_spec, cache_spec), check_vma=False)
```

time: 204 us -> 159 us (0.78)
  the two profiles are of different devices: /device:TPU:3 before, /device:TPU:0 now
where the time goes in v3:
time: 159 us
  Pallas kernels  145 us (91%)
  local copies, waits for them, and re-layouts  9.06 us (6%)
  other arithmetic  3.74 us (2%)
    pallas_call x1, Pallas kernels, local_layer(): pl.pallas_call(layer_kernel, in_specs=[hbm, vmem, vmem, vmem] + [hbm] * 7...  145 us
    unnamed x1, local copies, waits for them, and re-layouts  4.79 us
    reshape x2, local copies, waits for them, and re-layouts, local_layer(): return (out, k.reshape(shape), v.reshape(shape))  4.27 us

profile of v3, /device:TPU:0, one launch (start us, length us, event | category | flops | bytes accessed | tf_op | source)
XLA Modules:
  0.0 158.8 jit_solution(13088606494467953344)
XLA Ops:
  0.6 0.7 convert_element_type.10
  1.3 3.0 %fusion = (f32[1024,128]{1,0:T(8,128)}, f32[1024,128]{1,0:T(8,128)}) fusion(f32[128]{0:T(128)S(1)} %get-tuple-element.11, f32[128]{0:T(128)S(1)} %get-tuple-element.12, f32[1024]{0:T(1024)S(1)} %convert_element_type.10), kind=kLoop, calls=%fused_computation.2 | loop fusion | flops 262144 | bytes 1053696 | tf_op jit(solution)/shard_map/mul | solution.py:428
  4.4 145.3 %layer.1 = (bf16[1024,2048]{1,0:T(8,128)(2,1)}, bf16[1024,512]{1,0:T(8,128)(2,1)}, bf16[1024,512]{1,0:T(8,128)(2,1)}) custom-call(bf16[1024,2048]{1,0:T(8,128)(2,1)} %x_hbm.1, bf16[16,128]{1,0:T(8,128)(2,1)} %bitcast.1, f32[1024,128]{1,0:T(8,128)} %get-tuple-element.10.cos_ref, f32[1024,128]{1,0:T(8,128)} %get-tuple-element.9.sin_ref, ...), custom_call_target="tpu_custom_call" | custom-call | tf_op jit(solution)/shard_map/layer/pallas_call | solution.py:447
  149.7 2.1 %reshape.36 = bf16[1024,4,128]{2,1,0:T(4,128)(2,1)} reshape(bf16[1024,512]{1,0:T(8,128)(2,1)} %get-tuple-element.7) | data formatting | bytes 2097152 | tf_op jit(solution)/shard_map/reshape | solution.py:485
  151.8 2.1 %reshape.37 = bf16[1024,4,128]{2,1,0:T(4,128)(2,1)} reshape(bf16[1024,512]{1,0:T(8,128)(2,1)} %get-tuple-element.8) | data formatting | bytes 2097152 | tf_op jit(solution)/shard_map/reshape | solution.py:485
  154.0 4.8 %copy.14 = bf16[1024,2048]{1,0:T(8,128)(2,1)} copy(bf16[1024,2048]{1,0:T(8,128)(2,1)} %get-tuple-element.16) | data formatting | bytes 8388608
  (1 shorter events, 0.0 us)

commit v4 on v3

--- a/solution.py
+++ b/solution.py
@@ -3,6 +3,7 @@
 
 import jax
 import jax.numpy as jnp
+import numpy as np
 from jax import lax
 from jax.experimental import pallas as pl
 from jax.experimental.pallas import tpu as pltpu
@@ -21,16 +22,16 @@
 RBLK = 256
 CHUNK = 128
 KEYS = 512
-VIA = 1
-VIA_AFTER = 5
+VIA = 2
+VIA_AFTER = 6
 VIA_PIECES = 4
 
 
-def layer_kernel(x_hbm, gain_ref, cos_ref, sin_ref, wq_hbm, wk_hbm, wv_hbm, wo_hbm, wg_hbm, wu_hbm, wd_hbm,
+def layer_kernel(x_hbm, gain_ref, pos_ref, freq_ref, wq_hbm, wk_hbm, wv_hbm, wo_hbm, wg_hbm, wu_hbm, wd_hbm,
                  out_hbm, k_hbm, v_hbm,
                  x_buf, h_buf, ring, act, q_buf, k_all, vt_all, v_own, wo, wd, recv, mlp, qs, o_buf, s_ref, blk_ref, top_ref, sum_ref, acc_ref,
                  x_sem, ring_sem, wo_sem, wd_sem, kv_sem, out_sem,
-                 cross_send, cross_recv, up_send, up_recv, relay_send, relay_recv, part_send, part_recv, via, via_send, via_recv):
+                 cross_send, cross_recv, up_send, up_recv, relay_send, relay_recv, part_send, part_recv, via, via_send, via_recv, cos_ref, sin_ref, swap):
     me = lax.axis_index("cp")
     tp = lax.axis_index("tp")
     odd = me % 2
@@ -59,10 +60,10 @@
     w_copy(wv_hbm, 1, 1).start()
     for b in range(1, n_rblk):
         x_copy(b).start()
+    for j in range(4):
+        w_copy(wq_hbm, j, 4 + j).start()
     w_copy(wk_hbm, 0, 2).start()
     w_copy(wk_hbm, 1, 3).start()
-    for j in range(4):
-        w_copy(wq_hbm, j, 4 + j).start()
     wo_copy.start()
     wd_copy.start()
 
@@ -136,8 +137,12 @@
         h = h_buf[r, :]
         for j in range(2):
             v = jnp.dot(h, ring[j], preferred_element_type=F32).astype(BF16)
-            v_own[r, j * WBLK:(j + 1) * WBLK] = v
+            v_own[b % 2, :, j * WBLK:(j + 1) * WBLK] = v
             vt_all[j * WBLK:(j + 1) * WBLK, at] = v.T
+
+    def v_copy(b):
+        r = pl.ds(pl.multiple_of(b * RBLK, RBLK), RBLK)
+        return pltpu.make_async_copy(v_own.at[b % 2], v_hbm.at[r, :], kv_sem.at[b % 2])
 
     x_copy(0).wait()
     norm(0)
@@ -148,92 +153,107 @@
     @pl.loop(0, n_rblk - 1)
     def _(b):
         x_copy(b + 1).wait()
+
+        @pl.when(b >= 2)
+        def _():
+            v_copy(b - 2).wait()
+
         project_v(b)
         norm(b + 1)
         send_piece(0, b)
-
+        v_copy(b).start()
+
+    v_copy(n_rblk - 3).wait()
     project_v(n_rblk - 1)
     send_piece(0, n_rblk - 1)
-    v_out = pltpu.make_async_copy(v_own, v_hbm, kv_sem.at[0])
-    v_out.start()
+    v_copy(n_rblk - 1).start()
+
+    def ff_copies(s):
+        slot = 2 * (s % 4)
+        return w_copy(wg_hbm, s % n_ff, slot), w_copy(wu_hbm, s % n_ff, slot + 1)
+
+    def ff_start(s):
+        for copy in ff_copies(s):
+            copy.start()
+
+    ff_start(0)
+    sign = jnp.where(lax.broadcasted_iota(jnp.int32, (1, HEAD_DIM), 1) % 2 == 0, -1.0, 1.0).astype(F32)
+
+    @pl.loop(0, 4)
+    def _(j):
+        w_copy(wq_hbm, j, 4 + j).wait()
+        for b in range(n_rblk):
+            r = slice(b * RBLK, (b + 1) * RBLK)
+            cols = pl.ds(pl.multiple_of(j * WBLK, WBLK), WBLK)
+            q_buf[r, cols] = jnp.dot(h_buf[r, :], ring[4 + j], preferred_element_type=F32).astype(BF16)
+        for i in range(2):
+            row = 2 * j + i
+            pos = jnp.broadcast_to(pos_ref[pl.ds(row, 1), :].astype(F32), (HEAD_DIM, HEAD_DIM)).T
+            angle = pos * freq_ref[...]
+            at = pl.ds(pl.multiple_of(row * HEAD_DIM, HEAD_DIM), HEAD_DIM)
+            cos_ref[at, :] = jnp.cos(angle)
+            sin_ref[at, :] = jnp.sin(angle) * sign
+
+    ff_start(2)
+    ff_start(3)
 
     lane = lax.broadcasted_iota(jnp.int32, (WBLK, WBLK), 0)
     other = lax.broadcasted_iota(jnp.int32, (WBLK, WBLK), 1)
-    swap = jnp.where(lane == other + 1 - 2 * (other % 2), 1.0, 0.0).astype(BF16)
-
-    def rope_block(slot, dst, row0, col):
+    swap[...] = jnp.where(lane == other + 1 - 2 * (other % 2), 1.0, 0.0).astype(BF16)
+
+    def rotate(proj, swapped, r):
+        cos = cos_ref[r, :]
+        sin = sin_ref[r, :]
+        heads = [slice(i * HEAD_DIM, (i + 1) * HEAD_DIM) for i in range(WBLK // HEAD_DIM)]
+        return [(proj[:, c].astype(F32) * cos + swapped[:, c] * sin).astype(BF16) for c in heads]
+
+    @pl.loop(0, 2)
+    def _(j):
+        w_copy(wk_hbm, j, 2 + j).wait()
         proj = [None] * n_rblk
 
         def project(b):
-            proj[b] = jnp.dot(h_buf[b * RBLK:(b + 1) * RBLK, :], ring[slot], preferred_element_type=F32).astype(BF16)
+            proj[b] = jnp.dot(h_buf[b * RBLK:(b + 1) * RBLK, :], ring[2 + j], preferred_element_type=F32).astype(BF16)
 
         project(0)
         for b in range(n_rblk):
             if b + 1 < n_rblk:
                 project(b + 1)
-            r = slice(b * RBLK, (b + 1) * RBLK)
-            swapped = jnp.dot(proj[b], swap, preferred_element_type=F32)
-            cos = cos_ref[r, :]
-            sin = sin_ref[r, :]
-            halves = []
-            for i in range(WBLK // HEAD_DIM):
-                c = slice(i * HEAD_DIM, (i + 1) * HEAD_DIM)
-                halves.append((proj[b][:, c].astype(F32) * cos + swapped[:, c] * sin).astype(BF16))
-            at = pl.ds(pl.multiple_of(row0 + b * RBLK, RBLK), RBLK)
-            dst[at, pl.ds(pl.multiple_of(col, WBLK), WBLK)] = jnp.concatenate(halves, axis=1)
-
-    @pl.loop(0, 2)
-    def _(j):
-        w_copy(wk_hbm, j, 2 + j).wait()
-        rope_block(2 + j, k_all, me * rows, j * WBLK)
+            swapped = jnp.dot(proj[b], swap[...], preferred_element_type=F32)
+            at = pl.ds(pl.multiple_of(me * rows + b * RBLK, RBLK), RBLK)
+            cols = pl.ds(pl.multiple_of(j * WBLK, WBLK), WBLK)
+            k_all[at, cols] = jnp.concatenate(rotate(proj[b], swapped, slice(b * RBLK, (b + 1) * RBLK)), axis=1)
         send_piece(1, 2 * j)
         send_piece(1, 2 * j + 1)
 
-    k_out = pltpu.make_async_copy(k_all.at[pl.ds(pl.multiple_of(me * rows, RBLK), rows), :], k_hbm, kv_sem.at[1])
+    ff_start(1)
+    k_out = pltpu.make_async_copy(k_all.at[pl.ds(pl.multiple_of(me * rows, RBLK), rows), :], k_hbm, kv_sem.at[2])
     k_out.start()
 
-    def ff_copies(s):
-        slot = 2 * (s % 4)
-        return w_copy(wg_hbm, s % n_ff, slot), w_copy(wu_hbm, s % n_ff, slot + 1)
-
-    for s in range(2):
-        for copy in ff_copies(s):
-            copy.start()
-
-    @pl.loop(0, 4)
-    def _(j):
-        w_copy(wq_hbm, j, 4 + j).wait()
-        rope_block(4 + j, q_buf, 0, j * WBLK)
-
-    for s in range(2, 4):
-        for copy in ff_copies(s):
-            copy.start()
-
-    relay_steps = ((0, 0, 0), (2, 0, 1), (6, 0, 2), (10, 0, 3), (15, 1, 0), (19, 1, 1), (23, 1, 2))
-
-    def feed(half):
-        @pl.loop(half * n_ff, (half + 1) * n_ff)
+    relay_steps = ((12, 0, 0), (14, 0, 1), (18, 0, 2), (22, 0, 3), (27, 1, 0), (31, 1, 1), (35, 1, 2))
+    n_steps = 3 * n_ff
+
+    def feed(first_step, first_block, n_blocks):
+        @pl.loop(first_step, first_step + n_ff)
         def _(s):
             for copy in ff_copies(s):
                 copy.wait()
             slot = 2 * (s % 4)
-            for b in range(half * n_rblk // 2, (half + 1) * n_rblk // 2):
-                r = slice(b * RBLK, (b + 1) * RBLK)
+            for b in range(n_blocks):
+                r = pl.ds(pl.multiple_of((first_block + b) * RBLK, RBLK), RBLK)
                 h = h_buf[r, :]
                 gate = jnp.dot(h, ring[slot], preferred_element_type=F32).astype(BF16).astype(F32)
                 up_ = jnp.dot(h, ring[slot + 1], preferred_element_type=F32).astype(BF16).astype(F32)
                 act[r, pl.ds(pl.multiple_of((s % n_ff) * WBLK, WBLK), WBLK)] = (jax.nn.silu(gate) * up_).astype(BF16)
 
-            @pl.when(s + 4 < 2 * n_ff)
+            @pl.when(s + 4 < n_steps)
             def _():
-                for copy in ff_copies(s + 4):
-                    copy.start()
+                ff_start(s + 4)
 
             for step, kind, b in relay_steps:
-                if half * n_ff <= step < (half + 1) * n_ff:
-                    @pl.when((me >= 2) & (s == step))
-                    def _():
-                        relay_piece(kind, b)
+                @pl.when((me >= 2) & (s == step))
+                def _():
+                    relay_piece(kind, b)
 
     def down(c):
         r = pl.ds(pl.multiple_of(c * CHUNK, CHUNK), CHUNK)
@@ -269,10 +289,10 @@
 
     def chunk(c, stop):
         r = pl.ds(pl.multiple_of(c * CHUNK, CHUNK), CHUNK)
+        swapped = [jnp.dot(q_buf[r, g * WBLK:(g + 1) * WBLK], swap[...], preferred_element_type=F32) for g in range(kv_heads)]
         for g in range(kv_heads):
-            for i in range(2):
-                col = (2 * g + i) * HEAD_DIM
-                qs[g, i * CHUNK:(i + 1) * CHUNK, :] = q_buf[r, col:col + HEAD_DIM]
+            for i, q in enumerate(rotate(q_buf[r, g * WBLK:(g + 1) * WBLK], swapped[g], r)):
+                qs[g, i * CHUNK:(i + 1) * CHUNK, :] = q
         top_ref[...] = jnp.full_like(top_ref, -jnp.inf)
         sum_ref[...] = jnp.zeros_like(sum_ref)
         acc_ref[...] = jnp.zeros_like(acc_ref)
@@ -323,27 +343,41 @@
         def _():
             down(c + 1)
 
-    early = jnp.where(me < 2, n_chunk // 2, 0)
-    feed(0)
-    wo_copy.wait()
-    wd_copy.wait()
-
-    @pl.when(odd == 1)
+    per_block = RBLK // CHUNK
+    early = jnp.where(me < 2, 2, 0)
+
+    def await_weights():
+        wo_copy.wait()
+        wd_copy.wait()
+
+        @pl.when(odd == 1)
+        def _():
+            for kind in range(2):
+                for b in range(n_rblk):
+                    up(me - 1, kind, b).wait_recv()
+
+    @pl.loop(0, early)
+    def _(block):
+        feed(block * n_ff, block, 1)
+
+        @pl.when(block == 0)
+        def _():
+            await_weights()
+
+        first = block * per_block
+        down(first)
+
+        @pl.loop(first, first + per_block)
+        def _(c):
+            chunk(c, first + per_block)
+
+    @pl.when(me >= 2)
     def _():
-        for kind in range(2):
-            for b in range(n_rblk):
-                up(me - 1, kind, b).wait_recv()
-
-    @pl.when(me < 2)
-    def _():
-        down(0)
-
-    @pl.loop(0, early)
-    def _(c):
-        chunk(c, early)
-
-    feed(1)
-    down(early)
+        feed(n_ff, 0, 2)
+        await_weights()
+
+    feed(2 * n_ff, 2, 2)
+    down(early * per_block)
 
     @pl.when(me >= 2)
     def _():
@@ -352,7 +386,7 @@
             for b in range(n_rblk):
                 kv_copy(3 - me, kind, b, relay_send, relay_recv, partner).wait_recv()
 
-    @pl.loop(early, n_chunk)
+    @pl.loop(early * per_block, n_chunk)
     def _(c):
         chunk(c, n_chunk)
 
@@ -402,7 +436,8 @@
             via_copy(1, i).wait_send()
             via_copy(2, i).wait_send()
 
-    v_out.wait()
+    v_copy(n_rblk - 2).wait()
+    v_copy(n_rblk - 1).wait()
     k_out.wait()
     for kind in range(2):
         for b in range(n_rblk):
@@ -419,13 +454,27 @@
                 kv_copy(me - 2, kind, b, relay_send, relay_recv, partner).wait_send()
 
 
-def rope_tables(positions):
-    lane = jnp.arange(HEAD_DIM)
-    exponent = (lane - lane % 2).astype(F32) / HEAD_DIM
-    inv_freq = 1.0 / (ROPE_BASE ** exponent)
-    angles = positions.astype(F32)[:, None] * inv_freq[None, :]
-    sign = jnp.where(lane % 2 == 0, -1.0, 1.0).astype(F32)
-    return jnp.cos(angles), jnp.sin(angles) * sign[None, :]
+def place_kernel(m_ref, k_ref, v_ref, out_ref, kc_ref, vc_ref):
+    out_ref[...] = m_ref[...]
+    kc_ref[...] = k_ref[...].reshape(kc_ref.shape)
+    vc_ref[...] = v_ref[...].reshape(vc_ref.shape)
+
+
+def place(out, k, v, kv_heads):
+    rows, width = out.shape
+    blk = 256
+    kv_spec = pl.BlockSpec((blk, k.shape[1]), lambda i: (i, 0))
+    cache_spec = pl.BlockSpec((blk, kv_heads, HEAD_DIM), lambda i: (i, 0, 0))
+    cache = jax.ShapeDtypeStruct((rows, kv_heads, HEAD_DIM), BF16)
+    return pl.pallas_call(
+        place_kernel,
+        grid=(rows // blk,),
+        in_specs=[pl.BlockSpec((blk, width), lambda i: (i, 0)), kv_spec, kv_spec],
+        out_specs=[pl.BlockSpec((blk, width), lambda i: (i, 0)), cache_spec, cache_spec],
+        out_shape=[jax.ShapeDtypeStruct((rows, width), BF16), cache, cache],
+        compiler_params=pltpu.CompilerParams(dimension_semantics=("arbitrary",)),
+        name="place",
+    )(out, k, v)
 
 
 def solution(mesh):
@@ -440,7 +489,8 @@
         keys = n_cp * rows
         n_chunk = rows // CHUNK
         pieces = 2 * (rows // RBLK)
-        cos, sin = rope_tables(positions)
+        lane = np.arange(HEAD_DIM)
+        inv_freq = (1.0 / ROPE_BASE ** ((lane - lane % 2) / HEAD_DIM)).astype(np.float32)
         hbm = pl.BlockSpec(memory_space=pl.ANY)
         vmem = pl.BlockSpec(memory_space=pltpu.VMEM)
         dma = pltpu.SemaphoreType.DMA
@@ -461,7 +511,7 @@
                 pltpu.VMEM((rows, q_cols), BF16),
                 pltpu.VMEM((keys, kv_cols), BF16),
                 pltpu.VMEM((kv_cols, keys), BF16),
-                pltpu.VMEM((rows, kv_cols), BF16),
+                pltpu.VMEM((2, RBLK, kv_cols), BF16),
                 pltpu.VMEM((q_cols, width), BF16),
                 pltpu.VMEM((ff, width), BF16),
                 pltpu.VMEM((rows, width), BF16),
@@ -473,16 +523,16 @@
                 pltpu.VMEM((kv_heads, 1, 2 * CHUNK), F32),
                 pltpu.VMEM((kv_heads, 1, 2 * CHUNK), F32),
                 pltpu.VMEM((kv_heads, HEAD_DIM, 2 * CHUNK), F32),
-                dma((rows // RBLK,)), dma((RING,)), dma, dma, dma((2,)), dma((n_chunk,)),
+                dma((rows // RBLK,)), dma((RING,)), dma, dma, dma((3,)), dma((n_chunk,)),
                 dma((pieces,)), dma((pieces,)), dma((pieces,)), dma((pieces,)), dma((pieces,)), dma((pieces,)),
                 dma((n_chunk,)), dma((n_chunk,)),
                 pltpu.VMEM((2, CHUNK, width), BF16), dma((3 * VIA_PIECES,)), dma((3 * VIA_PIECES,)),
+                pltpu.VMEM((rows, HEAD_DIM), F32), pltpu.VMEM((rows, HEAD_DIM), F32), pltpu.VMEM((WBLK, WBLK), BF16),
             ],
             compiler_params=pltpu.CompilerParams(collective_id=0, has_side_effects=True, vmem_limit_bytes=VMEM_LIMIT),
             name="layer",
-        )(hidden, ln_gain.reshape(width // HEAD_DIM, HEAD_DIM), cos, sin, w_q, w_k, w_v, w_o, w_gate, w_up, w_down)
-        shape = (rows, kv_heads, HEAD_DIM)
-        return out, k.reshape(shape), v.reshape(shape)
+        )(hidden, ln_gain.reshape(width // HEAD_DIM, HEAD_DIM), positions.reshape(rows // HEAD_DIM, HEAD_DIM), jnp.asarray(inv_freq[None, :]), w_q, w_k, w_v, w_o, w_gate, w_up, w_down)
+        return place(out, k, v, kv_heads)
 
     row_spec = P(('dp', 'cp'), None)
     col_spec = P(None, 'tp')

time: 159 us -> 148 us (0.931)
  the two profiles are of different devices: /device:TPU:0 before, /device:TPU:3 now
where the time goes in v4:
time: 148 us; the launch traced here: 147 us
  Pallas kernels  147 us (99%)
    pallas_call x1, Pallas kernels, local_layer(): pl.pallas_call(layer_kernel, in_specs=[hbm, vmem, vmem, vmem] + [hbm] * 7...  141 us
    pallas_call x1, Pallas kernels, place(): pl.pallas_call(place_kernel, grid=(rows // blk,), in_specs=[pl.BlockSpec(...  5.8 us

profile of v4, /device:TPU:3, one launch (start us, length us, event | category | flops | bytes accessed | tf_op | source)
XLA Modules:
  0.0 147.5 jit_solution(12166622709989091540)
XLA Ops:
  0.6 141.0 %layer.1 = (bf16[1024,2048]{1,0:T(8,128)(2,1)}, bf16[1024,512]{1,0:T(8,128)(2,1)}, bf16[1024,512]{1,0:T(8,128)(2,1)}) custom-call(bf16[1024,2048]{1,0:T(8,128)(2,1)} %x_hbm.1, bf16[16,128]{1,0:T(8,128)(2,1)} %bitcast.2, s32[8,128]{1,0:T(8,128)} %bitcast.3, f32[1,128]{1,0:T(1,128)} %constant.2.clone.freq_ref, bf16[2048,1024]{1,0:T(8,128)(2,1)} %wq_hbm.1, ...), custom_call_target="tpu_custom_call" | custom-call | tf_op jit(solution)/shard_map/layer/pallas_call | solution.py:497
  141.7 5.8 %place.1 = (bf16[1024,2048]{1,0:T(8,128)(2,1)}, bf16[1024,4,128]{2,1,0:T(4,128)(2,1)}, bf16[1024,4,128]{2,1,0:T(4,128)(2,1)}) custom-call(bf16[1024,2048]{1,0:T(8,128)(2,1)} %get-tuple-element.6.m_ref, bf16[1024,512]{1,0:T(8,128)(2,1)} %get-tuple-element.7.k_ref, bf16[1024,512]{1,0:T(8,128)(2,1)} %get-tuple-element.8.v_ref), custom_call_target="tpu_custom_call" | custom-call | tf_op jit(solution)/shard_map/place/pallas_call | solution.py:469

commit v5 on v4

--- a/solution.py
+++ b/solution.py
@@ -20,11 +20,13 @@
 WBLK = 256
 RING = 8
 RBLK = 256
+VBLK = 128
 CHUNK = 128
 KEYS = 512
-VIA = 2
+VIA = 3
+VIA_EXTRA = 16
 VIA_AFTER = 6
-VIA_PIECES = 4
+VIA_PIECES = 9
 
 
 def layer_kernel(x_hbm, gain_ref, pos_ref, freq_ref, wq_hbm, wk_hbm, wv_hbm, wo_hbm, wg_hbm, wu_hbm, wd_hbm,
@@ -38,14 +40,16 @@
     partner = me + 1 - 2 * odd
     across = (me + 2) % 4
     rows, width = x_buf.shape
-    kv_heads = k_all.shape[1] // HEAD_DIM
+    kv_heads = k_all.shape[0]
     n_rblk = rows // RBLK
+    n_vblk = rows // VBLK
+    n_piece = (n_vblk, kv_heads)
     n_chunk = rows // CHUNK
     n_ff = act.shape[1] // WBLK
     part = h_buf
 
     def x_copy(b):
-        r = pl.ds(pl.multiple_of(b * RBLK, RBLK), RBLK)
+        r = pl.ds(pl.multiple_of(b * VBLK, VBLK), VBLK)
         return pltpu.make_async_copy(x_hbm.at[r, :], x_buf.at[r, :], x_sem.at[b])
 
     def w_copy(w_hbm, blk, slot):
@@ -58,7 +62,7 @@
     x_copy(0).start()
     w_copy(wv_hbm, 0, 0).start()
     w_copy(wv_hbm, 1, 1).start()
-    for b in range(1, n_rblk):
+    for b in range(1, n_vblk):
         x_copy(b).start()
     for j in range(4):
         w_copy(wq_hbm, j, 4 + j).start()
@@ -74,13 +78,12 @@
 
     def region(owner, kind, b):
         if kind:
-            at = pl.ds(pl.multiple_of(owner * rows + (b % 2) * (rows // 2), RBLK), rows // 2)
-            return k_all.at[at, pl.ds(pl.multiple_of((b // 2) * WBLK, WBLK), WBLK)]
-        return vt_all.at[:, pl.ds(pl.multiple_of(owner * rows + b * RBLK, RBLK), RBLK)]
+            return k_all.at[b, pl.ds(pl.multiple_of(owner * rows, RBLK), rows), :]
+        return vt_all.at[owner * n_vblk + b]
 
     def kv_copy(owner, kind, b, sends, recvs, target):
         ref = region(owner, kind, b)
-        i = kind * n_rblk + b
+        i = kind * n_vblk + b
         return pltpu.make_async_remote_copy(ref, ref, sends.at[i], recvs.at[i], device_id={"cp": target}, device_id_type=MESH)
 
     def cross(owner, kind, b):
@@ -106,15 +109,27 @@
         cross(owner, kind, b).wait_recv()
         kv_copy(owner, kind, b, relay_send, relay_recv, partner).start()
 
-    def part_copy(c):
-        r = pl.ds(pl.multiple_of(c * CHUNK, CHUNK), CHUNK)
+    def part_copy(c, n=CHUNK):
+        r = pl.ds(pl.multiple_of(c * CHUNK, CHUNK), n)
         return pltpu.make_async_remote_copy(part.at[r, :], recv.at[r, :], part_send.at[c], part_recv.at[c],
                                             device_id={"tp": 1 - tp}, device_id_type=MESH)
 
+    def for_part(c, act_on):
+        upper = me >= 2
+        short = upper & (c == VIA - 1)
+
+        @pl.when(short)
+        def _():
+            act_on(part_copy(VIA - 1, CHUNK - VIA_EXTRA))
+
+        @pl.when(jnp.logical_not(short | (upper & (c == VIA))))
+        def _():
+            act_on(part_copy(c))
+
     def via_copy(leg, i):
-        n = CHUNK // VIA_PIECES
+        n = VIA_EXTRA
         rows_i = slice(i * n, (i + 1) * n)
-        at = slice(VIA * CHUNK + i * n, VIA * CHUNK + (i + 1) * n)
+        at = slice(VIA * CHUNK + (i - 1) * n, VIA * CHUNK + i * n)
         src = (part.at[at, :], via.at[0, rows_i, :], via.at[1, rows_i, :])[leg]
         dst = (via.at[0, rows_i, :], via.at[1, rows_i, :], recv.at[at, :])[leg]
         target = {"tp": 1 - tp} if leg == 1 else {"cp": across}
@@ -124,7 +139,7 @@
     gain = jnp.concatenate([gain_ref[i:i + 1, :] for i in range(width // HEAD_DIM)], axis=1).astype(F32)
 
     def norm(b):
-        r = pl.ds(pl.multiple_of(b * RBLK, RBLK), RBLK)
+        r = pl.ds(pl.multiple_of(b * VBLK, VBLK), VBLK)
         x = x_buf[r, :].astype(F32)
         mean = jnp.mean(x, axis=-1, keepdims=True)
         cent = x - mean
@@ -132,16 +147,15 @@
         h_buf[r, :] = (cent * lax.rsqrt(var + LN_EPS) * gain).astype(BF16)
 
     def project_v(b):
-        r = pl.ds(pl.multiple_of(b * RBLK, RBLK), RBLK)
-        at = pl.ds(pl.multiple_of(me * rows + b * RBLK, RBLK), RBLK)
+        r = pl.ds(pl.multiple_of(b * VBLK, VBLK), VBLK)
         h = h_buf[r, :]
         for j in range(2):
             v = jnp.dot(h, ring[j], preferred_element_type=F32).astype(BF16)
             v_own[b % 2, :, j * WBLK:(j + 1) * WBLK] = v
-            vt_all[j * WBLK:(j + 1) * WBLK, at] = v.T
+            vt_all[me * n_vblk + b, j * WBLK:(j + 1) * WBLK, :] = v.T
 
     def v_copy(b):
-        r = pl.ds(pl.multiple_of(b * RBLK, RBLK), RBLK)
+        r = pl.ds(pl.multiple_of(b * VBLK, VBLK), VBLK)
         return pltpu.make_async_copy(v_own.at[b % 2], v_hbm.at[r, :], kv_sem.at[b % 2])
 
     x_copy(0).wait()
@@ -150,7 +164,7 @@
     w_copy(wv_hbm, 1, 1).wait()
     pl.semaphore_wait(barrier, 3)
 
-    @pl.loop(0, n_rblk - 1)
+    @pl.loop(0, n_vblk - 1)
     def _(b):
         x_copy(b + 1).wait()
 
@@ -163,10 +177,10 @@
         send_piece(0, b)
         v_copy(b).start()
 
-    v_copy(n_rblk - 3).wait()
-    project_v(n_rblk - 1)
-    send_piece(0, n_rblk - 1)
-    v_copy(n_rblk - 1).start()
+    v_copy(n_vblk - 3).wait()
+    project_v(n_vblk - 1)
+    send_piece(0, n_vblk - 1)
+    v_copy(n_vblk - 1).start()
 
     def ff_copies(s):
         slot = 2 * (s % 4)
@@ -221,16 +235,21 @@
                 project(b + 1)
             swapped = jnp.dot(proj[b], swap[...], preferred_element_type=F32)
             at = pl.ds(pl.multiple_of(me * rows + b * RBLK, RBLK), RBLK)
-            cols = pl.ds(pl.multiple_of(j * WBLK, WBLK), WBLK)
-            k_all[at, cols] = jnp.concatenate(rotate(proj[b], swapped, slice(b * RBLK, (b + 1) * RBLK)), axis=1)
+            for i, k in enumerate(rotate(proj[b], swapped, slice(b * RBLK, (b + 1) * RBLK))):
+                k_all[2 * j + i, at, :] = k
         send_piece(1, 2 * j)
         send_piece(1, 2 * j + 1)
 
     ff_start(1)
-    k_out = pltpu.make_async_copy(k_all.at[pl.ds(pl.multiple_of(me * rows, RBLK), rows), :], k_hbm, kv_sem.at[2])
-    k_out.start()
-
-    relay_steps = ((12, 0, 0), (14, 0, 1), (18, 0, 2), (22, 0, 3), (27, 1, 0), (31, 1, 1), (35, 1, 2))
+    def k_copy(g):
+        return pltpu.make_async_copy(k_all.at[g, pl.ds(pl.multiple_of(me * rows, RBLK), rows), :],
+                                     k_hbm.at[:, g * HEAD_DIM:(g + 1) * HEAD_DIM], kv_sem.at[2 + g])
+
+    for g in range(kv_heads):
+        k_copy(g).start()
+
+    relay_steps = ((12, 0, 0), (12, 0, 1), (12, 0, 2), (12, 0, 3), (14, 0, 4), (16, 0, 5), (19, 0, 6), (21, 0, 7),
+                   (26, 1, 0), (30, 1, 1), (34, 1, 2))
     n_steps = 3 * n_ff
 
     def feed(first_step, first_block, n_blocks):
@@ -264,6 +283,8 @@
 
     scale = HEAD_DIM ** -0.5 * math.log2(math.e)
 
+    low = jnp.where(me < 2, 0, 2 * (rows // KEYS))
+
     def head(g):
         return slice(g * HEAD_DIM, (g + 1) * HEAD_DIM)
 
@@ -271,7 +292,7 @@
         return pl.ds(pl.multiple_of(j * KEYS, KEYS), KEYS)
 
     def score(j, g):
-        s = lax.dot_general(k_all[key_rows(j), head(g)], qs[g], (((1,), (1,)), ((), ())), preferred_element_type=F32)
+        s = lax.dot_general(k_all[g, key_rows(j), :], qs[g], (((1,), (1,)), ((), ())), preferred_element_type=F32)
         s_ref[g] = s
         blk_ref[g] = jnp.max(s, axis=0, keepdims=True)
 
@@ -285,7 +306,8 @@
         return factor, weight.astype(BF16)
 
     def collect(j, g, factor, weight):
-        acc_ref[g] = acc_ref[g] * factor + jnp.dot(vt_all[head(g), key_rows(j)], weight, preferred_element_type=F32)
+        vt = jnp.concatenate([vt_all[j * (KEYS // VBLK) + i, head(g), :] for i in range(KEYS // VBLK)], axis=1)
+        acc_ref[g] = acc_ref[g] * factor + jnp.dot(vt, weight, preferred_element_type=F32)
 
     def chunk(c, stop):
         r = pl.ds(pl.multiple_of(c * CHUNK, CHUNK), CHUNK)
@@ -298,14 +320,17 @@
         acc_ref[...] = jnp.zeros_like(acc_ref)
         full = me * (rows // KEYS) + c // (KEYS // CHUNK)
         for g in range(kv_heads):
-            score(0, g)
-
-        @pl.loop(0, full)
-        def _(j):
+            score(low, g)
+
+        def step(j):
             for g in range(kv_heads):
                 factor, weight = weigh(g, s_ref[g], blk_ref[g])
                 score(j + 1, g)
                 collect(j, g, factor, weight)
+
+        @pl.loop(low, full)
+        def _(j):
+            step(j)
 
         first = (c % (KEYS // CHUNK)) * CHUNK
         key_id = lax.broadcasted_iota(jnp.int32, (KEYS, 2 * CHUNK), 0)
@@ -314,6 +339,23 @@
             s = jnp.where(key_id <= query_id + first, s_ref[g], -jnp.inf)
             factor, weight = weigh(g, s, jnp.max(s, axis=0, keepdims=True))
             collect(full, g, factor, weight)
+
+        @pl.when(me >= 2)
+        def _():
+            @pl.when(c == 0)
+            def _():
+                relay_piece(1, 3)
+                for kind in range(2):
+                    for b in range(n_piece[kind]):
+                        kv_copy(3 - me, kind, b, relay_send, relay_recv, partner).wait_recv()
+
+            for g in range(kv_heads):
+                score(0, g)
+
+            @pl.loop(0, low)
+            def _(j):
+                step(j)
+
         for g in range(kv_heads):
             o = (acc_ref[g] / sum_ref[g]).T.astype(BF16)
             for i in range(2):
@@ -324,13 +366,15 @@
             cols = slice(j * (width // 4), (j + 1) * (width // 4))
             part[r, cols] = (jnp.dot(o, wo[:, cols], preferred_element_type=F32) + mlp[:, cols]).astype(BF16)
 
-        @pl.when((me < 2) | (c != VIA))
-        def _():
-            part_copy(c).start()
+        for_part(c, lambda copy: copy.start())
+
+        @pl.when((me >= 2) & (c == VIA - 1))
+        def _():
+            via_copy(0, 0).start()
 
         @pl.when((me >= 2) & (c == VIA))
         def _():
-            for i in range(VIA_PIECES):
+            for i in range(1, VIA_PIECES):
                 via_copy(0, i).start()
 
         @pl.when((me < 2) & (c == VIA_AFTER))
@@ -353,7 +397,7 @@
         @pl.when(odd == 1)
         def _():
             for kind in range(2):
-                for b in range(n_rblk):
+                for b in range(n_piece[kind]):
                     up(me - 1, kind, b).wait_recv()
 
     @pl.loop(0, early)
@@ -379,13 +423,6 @@
     feed(2 * n_ff, 2, 2)
     down(early * per_block)
 
-    @pl.when(me >= 2)
-    def _():
-        relay_piece(1, 3)
-        for kind in range(2):
-            for b in range(n_rblk):
-                kv_copy(3 - me, kind, b, relay_send, relay_recv, partner).wait_recv()
-
     @pl.loop(early * per_block, n_chunk)
     def _(c):
         chunk(c, n_chunk)
@@ -411,20 +448,20 @@
         def _():
             for i in range(VIA_PIECES):
                 via_copy(2, i).wait_recv()
+            finish(VIA - 1)
             finish(VIA)
 
-        @pl.when((me < 2) | (c != VIA))
-        def _():
-            part_copy(c).wait_recv()
+        for_part(c, lambda copy: copy.wait_recv())
+
+        @pl.when((me < 2) | ((c != VIA) & (c != VIA - 1)))
+        def _():
             finish(c)
 
     @pl.loop(0, n_chunk)
     def _(c):
         out_copy(c).wait()
 
-        @pl.when((me < 2) | (c != VIA))
-        def _():
-            part_copy(c).wait_send()
+        for_part(c, lambda copy: copy.wait_send())
 
     for i in range(VIA_PIECES):
         @pl.when(me >= 2)
@@ -436,11 +473,12 @@
             via_copy(1, i).wait_send()
             via_copy(2, i).wait_send()
 
-    v_copy(n_rblk - 2).wait()
-    v_copy(n_rblk - 1).wait()
-    k_out.wait()
+    v_copy(n_vblk - 2).wait()
+    v_copy(n_vblk - 1).wait()
+    for g in range(kv_heads):
+        k_copy(g).wait()
     for kind in range(2):
-        for b in range(n_rblk):
+        for b in range(n_piece[kind]):
             @pl.when(me < 2)
             def _():
                 cross(me, kind, b).wait_send()
@@ -462,7 +500,7 @@
 
 def place(out, k, v, kv_heads):
     rows, width = out.shape
-    blk = 256
+    blk = 512
     kv_spec = pl.BlockSpec((blk, k.shape[1]), lambda i: (i, 0))
     cache_spec = pl.BlockSpec((blk, kv_heads, HEAD_DIM), lambda i: (i, 0, 0))
     cache = jax.ShapeDtypeStruct((rows, kv_heads, HEAD_DIM), BF16)
@@ -488,7 +526,7 @@
         kv_heads = kv_cols // HEAD_DIM
         keys = n_cp * rows
         n_chunk = rows // CHUNK
-        pieces = 2 * (rows // RBLK)
+        pieces = rows // VBLK + kv_heads
         lane = np.arange(HEAD_DIM)
         inv_freq = (1.0 / ROPE_BASE ** ((lane - lane % 2) / HEAD_DIM)).astype(np.float32)
         hbm = pl.BlockSpec(memory_space=pl.ANY)
@@ -509,9 +547,9 @@
                 pltpu.VMEM((RING, width, WBLK), BF16),
                 pltpu.VMEM((rows, ff), BF16),
                 pltpu.VMEM((rows, q_cols), BF16),
-                pltpu.VMEM((keys, kv_cols), BF16),
-                pltpu.VMEM((kv_cols, keys), BF16),
-                pltpu.VMEM((2, RBLK, kv_cols), BF16),
+                pltpu.VMEM((kv_heads, keys, HEAD_DIM), BF16),
+                pltpu.VMEM((keys // VBLK, kv_cols, VBLK), BF16),
+                pltpu.VMEM((2, VBLK, kv_cols), BF16),
                 pltpu.VMEM((q_cols, width), BF16),
                 pltpu.VMEM((ff, width), BF16),
                 pltpu.VMEM((rows, width), BF16),
@@ -523,10 +561,10 @@
                 pltpu.VMEM((kv_heads, 1, 2 * CHUNK), F32),
                 pltpu.VMEM((kv_heads, 1, 2 * CHUNK), F32),
                 pltpu.VMEM((kv_heads, HEAD_DIM, 2 * CHUNK), F32),
-                dma((rows // RBLK,)), dma((RING,)), dma, dma, dma((3,)), dma((n_chunk,)),
+                dma((rows // VBLK,)), dma((RING,)), dma, dma, dma((2 + kv_heads,)), dma((n_chunk,)),
                 dma((pieces,)), dma((pieces,)), dma((pieces,)), dma((pieces,)), dma((pieces,)), dma((pieces,)),
                 dma((n_chunk,)), dma((n_chunk,)),
-                pltpu.VMEM((2, CHUNK, width), BF16), dma((3 * VIA_PIECES,)), dma((3 * VIA_PIECES,)),
+                pltpu.VMEM((2, VIA_EXTRA * VIA_PIECES, width), BF16), dma((3 * VIA_PIECES,)), dma((3 * VIA_PIECES,)),
                 pltpu.VMEM((rows, HEAD_DIM), F32), pltpu.VMEM((rows, HEAD_DIM), F32), pltpu.VMEM((WBLK, WBLK), BF16),
             ],
             compiler_params=pltpu.CompilerParams(collective_id=0, has_side_effects=True, vmem_limit_bytes=VMEM_LIMIT),

time: 148 us -> 146 us (0.986)
  the two profiles are of different devices: /device:TPU:3 before, /device:TPU:0 now
where the time goes in v5:
time: 146 us; the launch traced here: 144 us
  Pallas kernels  143 us (98%)
    pallas_call x1, Pallas kernels, local_layer(): pl.pallas_call(layer_kernel, in_specs=[hbm, vmem, vmem, vmem] + [hbm] * 7...  139 us
    pallas_call x1, Pallas kernels, place(): pl.pallas_call(place_kernel, grid=(rows // blk,), in_specs=[pl.BlockSpec(...  4.73 us

profile of v5, /device:TPU:0, one launch (start us, length us, event | category | flops | bytes accessed | tf_op | source)
XLA Modules:
  0.0 144.0 jit_solution(17009488513599711470)
XLA Ops:
  0.6 138.6 %layer.1 = (bf16[1024,2048]{1,0:T(8,128)(2,1)}, bf16[1024,512]{1,0:T(8,128)(2,1)}, bf16[1024,512]{1,0:T(8,128)(2,1)}) custom-call(bf16[1024,2048]{1,0:T(8,128)(2,1)} %x_hbm.1, bf16[16,128]{1,0:T(8,128)(2,1)} %bitcast.2, s32[8,128]{1,0:T(8,128)} %bitcast.3, f32[1,128]{1,0:T(1,128)} %constant.2.clone.freq_ref, bf16[2048,1024]{1,0:T(8,128)(2,1)} %wq_hbm.1, ...), custom_call_target="tpu_custom_call" | custom-call | tf_op jit(solution)/shard_map/layer/pallas_call | solution.py:535
  139.3 4.7 %place.1 = (bf16[1024,2048]{1,0:T(8,128)(2,1)}, bf16[1024,4,128]{2,1,0:T(4,128)(2,1)}, bf16[1024,4,128]{2,1,0:T(4,128)(2,1)}) custom-call(bf16[1024,2048]{1,0:T(8,128)(2,1)} %get-tuple-element.6.m_ref, bf16[1024,512]{1,0:T(8,128)(2,1)} %get-tuple-element.7.k_ref, bf16[1024,512]{1,0:T(8,128)(2,1)} %get-tuple-element.8.v_ref), custom_call_target="tpu_custom_call" | custom-call | tf_op jit(solution)/shard_map/place/pallas_call | solution.py:507

commit v6 on v5

--- a/solution.py
+++ b/solution.py
@@ -432,9 +432,11 @@
         return pltpu.make_async_copy(x_buf.at[r, :], out_hbm.at[r, :], out_sem.at[c])
 
     def finish(c):
-        r = pl.ds(pl.multiple_of(c * CHUNK, CHUNK), CHUNK)
-        x_buf[r, :] = (x_buf[r, :].astype(F32) + (part[r, :].astype(F32) + recv[r, :].astype(F32))).astype(BF16)
-        out_copy(c).start()
+        for i in range(4):
+            n = CHUNK // 4
+            r = pl.ds(pl.multiple_of(c * CHUNK + i * n, n), n)
+            x_buf[r, :] = (x_buf[r, :].astype(F32) + (part[r, :].astype(F32) + recv[r, :].astype(F32))).astype(BF16)
+            pltpu.make_async_copy(x_buf.at[r, :], out_hbm.at[r, :], out_sem.at[c]).start()
 
     @pl.loop(0, n_chunk)
     def _(c):

time: 146 us -> 146 us (level)
  no operation moved by 1% of the time
where the time goes in v6:
time: 146 us; the launch traced here: 144 us
  Pallas kernels  143 us (98%)
    pallas_call x1, Pallas kernels, local_layer(): pl.pallas_call(layer_kernel, in_specs=[hbm, vmem, vmem, vmem] + [hbm] * 7...  139 us
    pallas_call x1, Pallas kernels, place(): pl.pallas_call(place_kernel, grid=(rows // blk,), in_specs=[pl.BlockSpec(...  4.73 us

profile of v6, /device:TPU:0, one launch (start us, length us, event | category | flops | bytes accessed | tf_op | source)
XLA Modules:
  0.0 144.0 jit_solution(7871913682667460949)
XLA Ops:
  0.6 138.6 %layer.1 = (bf16[1024,2048]{1,0:T(8,128)(2,1)}, bf16[1024,512]{1,0:T(8,128)(2,1)}, bf16[1024,512]{1,0:T(8,128)(2,1)}) custom-call(bf16[1024,2048]{1,0:T(8,128)(2,1)} %x_hbm.1, bf16[16,128]{1,0:T(8,128)(2,1)} %bitcast.2, s32[8,128]{1,0:T(8,128)} %bitcast.3, f32[1,128]{1,0:T(1,128)} %constant.2.clone.freq_ref, bf16[2048,1024]{1,0:T(8,128)(2,1)} %wq_hbm.1, ...), custom_call_target="tpu_custom_call" | custom-call | tf_op jit(solution)/shard_map/layer/pallas_call | solution.py:537
  139.2 4.7 %place.1 = (bf16[1024,2048]{1,0:T(8,128)(2,1)}, bf16[1024,4,128]{2,1,0:T(4,128)(2,1)}, bf16[1024,4,128]{2,1,0:T(4,128)(2,1)}) custom-call(bf16[1024,2048]{1,0:T(8,128)(2,1)} %get-tuple-element.6.m_ref, bf16[1024,512]{1,0:T(8,128)(2,1)} %get-tuple-element.7.k_ref, bf16[1024,512]{1,0:T(8,128)(2,1)} %get-tuple-element.8.v_ref), custom_call_target="tpu_custom_call" | custom-call | tf_op jit(solution)/shard_map/place/pallas_call | solution.py:509
